TPU v7x, 256 devices: a whole 4x4x8 slice. The times are simulated.
256 devices in a mesh: span: 8 (over y, core), chord: 32 (over z, x).
Axes of the slice: x: 4, y: 4, z: 8, core: 2. Of those that a mesh axis runs over, the one named last changes fastest.
Arguments:
- node_pos: float32 [3, 524288], P(None, ('span', 'chord')), may hold values from -0.4 to 0.4
- ctrl_pos: float32 [3, 8192], P(None, ('span', 'chord')), may hold values from -0.4 to 0.4
- ctrl_ids: int32 [8192], P(('span', 'chord')), may hold values from 0 to 1023
- wing_shift: float32 [15, 1024], replicated, may hold values from -0.06 to 0.06
- wing_speed: float32 [15, 1024], replicated, may hold values from -0.6 to 0.6
- minv: float32 [8192, 8192], P(('span', 'chord')), may hold values from -1 to 3, as said below
- conn: int32 [64, 32768], P(None, ('span', 'chord')), may hold values from 0 to 2047
- face_elem: int32 [8, 32, 4, 32], P('span', 'chord'), may hold values from 0 to 127
- face_match: int32 [8, 32, 4, 32], P('span', 'chord'), may hold values from 0 to 31, each once within a row
Outputs:
- det_jac: float32 [5, 64, 32768], P(None, None, ('span', 'chord'))
- grid_flux: float32 [5, 3, 64, 32768], P(None, None, None, ('span', 'chord'))
- face_flux: float32 [8, 32, 4, 5, 16, 32], P('span', 'chord')
Inputs may be any that keep to these rules, and one draw needn't show every extreme that they name: minv is exactly symmetric. Each face_match[j, k, t, :] is a permutation of 0 to 31.
All inputs are finite; a program needn't handle non-finite values.
Results may differ from a plain program's by a relative error of at most 0.00025.
Values sent between devices are 32-bit elements; how exact they have to be, the bound alone decides.
A program may use at most 64 MiB of HBM per device.

v0:
```python
import math

import jax
import jax.numpy as jnp
import numpy as np
from jax import lax
from jax.sharding import Mesh
from jax.sharding import PartitionSpec as P

SPAN_CHORD = ("span_0", "span_1", "chord_0", "chord_1")
SPAN = ("span_0", "span_1")
CHORD = ("chord_0", "chord_1")


kernel_width = 0.1


def in_order(parts, dim):
    shape = list(parts.shape[1:])
    shape[dim] *= parts.shape[0]
    return jnp.moveaxis(parts, 0, dim).reshape(shape)


def stacked_from(shard, axes, sequence):
    parts = shard
    for k in sequence:
        parts = lax.all_gather(parts, axes[k])
    done = sequence[::-1]
    back = [done.index(k) for k in range(len(axes))]
    parts = parts.transpose(*back, *range(len(axes), parts.ndim))
    return parts.reshape(-1, *shard.shape)


def gather_axes(shard, axes, sequence, dim):
    return in_order(stacked_from(shard, axes, sequence), dim)


def gather_turned(arrays, axis, dims):
    turned = [jnp.moveaxis(a, dim, 0) for a, dim in zip(arrays, dims)]
    widths = [t[0].size for t in turned]
    both = jnp.concatenate([t.reshape(-1, w) for t, w in zip(turned, widths)], axis=1)
    whole = lax.all_gather(both, axis, axis=0, tiled=True)
    parts = jnp.split(whole, [sum(widths[:k]) for k in range(1, len(widths))], axis=1)
    return tuple(
        (
            jnp.moveaxis(b.reshape(-1, *t.shape[1:]), 0, dim)
            for b, t, dim in zip(parts, turned, dims)
        )
    )


def passed_along(block, axis, distance):
    devices = range(lax.axis_size(axis))
    route = [(i - distance, i) for i in devices if i - distance in devices]
    return lax.ppermute(block, axis, route)


def passed_along_2(value, axis, steps):
    count = lax.axis_size(axis)
    pairs = [(source, (source + steps) % count) for source in range(count)]
    return lax.ppermute(value, axis, pairs)


def lobatto_table():
    points = np.array([-1.0, -1.0 / np.sqrt(5.0), 1.0 / np.sqrt(5.0), 1.0])
    barycentric = np.array(
        [
            1.0
            / np.prod([points[target] - points[source] for source in range(4) if source != target])
            for target in range(4)
        ]
    )
    derivative = np.zeros((4, 4))
    for target in range(4):
        for source in range(4):
            if source != target:
                derivative[target, source] = (
                    barycentric[source] / barycentric[target] / (points[target] - points[source])
                )
        derivative[target, target] = -np.sum(derivative[target])
    identity = np.eye(4)
    stacked = np.stack(
        [
            np.kron(np.kron(derivative, identity), identity),
            np.kron(np.kron(identity, derivative), identity),
            np.kron(np.kron(identity, identity), derivative),
        ]
    )
    return stacked.reshape(192, 64)


def element_metrics(node_rows, positions, links):
    sections = node_rows.shape[0] // 6
    elements = links.shape[1]
    moved = node_rows[: 3 * sections] + jnp.tile(positions, (sections, 1))
    gathered = jnp.take(jnp.concatenate([moved, node_rows[3 * sections :]], axis=0), links, axis=1)
    table = jnp.asarray(lobatto_table(), jnp.float32)
    jacobian = jnp.einsum(
        "rq,kqe->rke", table, gathered[: 3 * sections], precision=lax.Precision.HIGHEST
    )
    jacobian = jacobian.reshape(3, 64, sections, 3, elements).transpose(2, 3, 0, 1, 4)
    velocity = gathered[3 * sections :].reshape(sections, 3, 64, elements)

    def entry(spatial, along):
        return jacobian[:, spatial % 3, along % 3]

    metric = [
        [
            entry(spatial + 1, along + 1) * entry(spatial + 2, along + 2)
            - entry(spatial + 1, along + 2) * entry(spatial + 2, along + 1)
            for spatial in range(3)
        ]
        for along in range(3)
    ]
    volume = entry(0, 0) * metric[0][0] + entry(0, 1) * metric[1][0] + entry(0, 2) * metric[2][0]
    flux = jnp.stack(
        [
            metric[along][0] * velocity[:, 0]
            + metric[along][1] * velocity[:, 1]
            + metric[along][2] * velocity[:, 2]
            for along in range(3)
        ],
        axis=1,
    )
    return (volume, flux)


def face_traces(flux, sides):
    sections, elements = (flux.shape[0], flux.shape[3])
    cube = flux.reshape(sections, 3, 4, 4, 4, elements)
    surfaces = [-cube[:, 2, :, :, 0], cube[:, 2, :, :, 3], -cube[:, 1, :, 0], cube[:, 1, :, 3]]
    return jnp.stack(
        [
            jnp.take(surface.reshape(sections, 16, elements), sides[ordinal], axis=2)
            for ordinal, surface in enumerate(surfaces)
        ]
    )


def kernel_sum(weights_piece, points_piece, nodes):
    columns = points_piece.shape[1]
    block_width = math.gcd(columns, 256)

    def step(counter, total):
        offset = counter * block_width
        weight_block = lax.dynamic_slice_in_dim(weights_piece, offset, block_width, 1)
        point_block = lax.dynamic_slice_in_dim(points_piece, offset, block_width, 1)
        distance = (
            (point_block[0][:, None] - nodes[0][None, :]) ** 2
            + (point_block[1][:, None] - nodes[1][None, :]) ** 2
            + (point_block[2][:, None] - nodes[2][None, :]) ** 2
        )
        kernel = jnp.exp(-distance / (2.0 * kernel_width**2))
        return total + jnp.dot(
            weight_block,
            kernel,
            precision=lax.Precision.HIGHEST,
            preferred_element_type=jnp.float32,
        )

    empty = jnp.zeros((weights_piece.shape[0], nodes.shape[1]), jnp.float32)
    return lax.fori_loop(0, columns // block_width, step, empty)


def on_device(
    node_pos, ctrl_pos, ctrl_ids, wing_shift, wing_speed, minv, conn, face_elem, face_match
):
    highest = lax.Precision.HIGHEST
    table = jnp.concatenate([wing_shift, wing_speed], axis=0)
    every_id = gather_axes(ctrl_ids, SPAN_CHORD, (0, 2, 3, 1), 0)
    right_side = jnp.take(table, every_id, axis=1)
    own_weights = lax.dot_general(
        right_side,
        minv,
        (((1,), (1,)), ((), ())),
        precision=highest,
        preferred_element_type=jnp.float32,
    )
    pieces = gather_turned((own_weights, ctrl_pos), SPAN_CHORD, (1, 1))
    motion = kernel_sum(pieces[0], pieces[1], node_pos)
    volume, flux = element_metrics(motion, node_pos, conn)
    own = face_traces(flux, face_elem[0, 0])
    lower = passed_along(own[1], SPAN, 1)
    upper = passed_along(own[0], SPAN, -1)
    before = passed_along_2(own[3], CHORD, 1)
    after = passed_along_2(own[2], CHORD, -1)
    received = jnp.stack([lower, upper, before, after])
    matched = jnp.stack(
        [jnp.take(received[ordinal], face_match[0, 0, ordinal], axis=2) for ordinal in range(4)]
    )
    position = lax.axis_index(SPAN)
    span_count = lax.axis_size(SPAN)
    side_index = jnp.arange(4, dtype=jnp.int32)
    boundary = (side_index == 0) & (position == 0) | (side_index == 1) & (
        position == span_count - 1
    )
    opposite = jnp.where(boundary[:, None, None, None], -own, matched)
    face_flux = (0.5 * (own - opposite))[None, None]
    return (volume, flux, face_flux)


def solution(mesh):
    split = Mesh(mesh.devices.reshape(4, 2, 8, 4), ("span_0", "span_1", "chord_0", "chord_1"))
    return jax.shard_map(
        on_device,
        mesh=split,
        in_specs=(
            P(None, SPAN_CHORD),
            P(None, SPAN_CHORD),
            P(SPAN_CHORD),
            P(),
            P(),
            P(SPAN_CHORD, None),
            P(None, SPAN_CHORD),
            P(SPAN, CHORD, None, None),
            P(SPAN, CHORD, None, None),
        ),
        out_specs=(
            P(None, None, SPAN_CHORD),
            P(None, None, None, SPAN_CHORD),
            P(SPAN, CHORD, None, None, None, None),
        ),
        check_vma=False,
    )
```

profile of v0, /device:TPU:1, one launch (start us, length us, event | category | flops | bytes accessed | tf_op | source)
XLA Modules:
  0.0 360.8 jit_solution(5451668358771411971)
XLA Ops:
  7.2 1.3 dynamic-slice
  9.2 0.9 dynamic-update-slice
  10.1 7.8 %all-reduce = s32[128]{0:T(128)S(1)} all-reduce(s32[128]{0:T(128)S(1)} %dynamic-update-slice), channel_id=2, replica_groups=mesh['span_0'=4,'span_1'=2,'chord_0'=8,'chord_1'=4] {'span_0'}, use_global_device_ids=true, to_apply=%add | all-reduce | flops 128 | bytes 1024
  18.0 19.8 %all-gather.4 = s32[8,4,32]{2,1,0:T(4,128)S(1)} all-gather(s32[1,4,32]{2,1,0:T(4,128)S(1)} %reshape.722), channel_id=3, replica_groups=mesh['span_0'=4,'span_1'=2,'chord_0'=8,'chord_1'=4] {'chord_0'}, dimensions={0}, use_global_device_ids=true | all-gather | bytes 4608 | tf_op jit(solution)/shard_map/all_gather | solution.py:27
  37.8 9.3 %all-gather.2 = s32[32,4,32]{2,1,0:T(4,128)S(1)} all-gather(s32[8,4,32]{2,1,0:T(4,128)S(1)} %all-gather.4), channel_id=4, replica_groups=mesh['span_0'=4,'span_1'=2,'chord_0'=8,'chord_1'=4] {'chord_1'}, dimensions={0}, use_global_device_ids=true | all-gather | bytes 20480 | tf_op jit(solution)/shard_map/all_gather | solution.py:27
  47.1 12.9 %all-gather.3 = s32[8,8,4,32]{3,1,2,0:T(8,128)S(1)} all-gather(s32[4,8,4,32]{3,1,2,0:T(8,128)S(1)} %copy.78), channel_id=5, replica_groups=mesh['span_0'=4,'span_1'=2,'chord_0'=8,'chord_1'=4] {'span_1'}, dimensions={0}, use_global_device_ids=true | all-gather | bytes 49152 | tf_op jit(solution)/shard_map/all_gather | solution.py:27
  60.5 0.9 pad_maximum_fusion.3
  61.6 27.7 %gather_fusion = f32[8192,30]{1,0:T(8,128)} fusion(f32[30,1024]{0,1:T(8,128)S(1)} %copy.81, s32[8192]{0:T(1024)S(1)} %broadcast_clamp_fusion), kind=kCustom, calls=%fused_computation.8 | custom fusion | bytes 1998848 | tf_op jit(solution)/shard_map/jit(_take)/gather | solution.py:171
  89.3 10.0 %fusion.25 = f32[32,30]{0,1:T(8,128)S(1)} fusion(f32[32,8192]{1,0:T(8,128)S(1)} %copy-done, f32[8192,30]{1,0:T(8,128)} %gather_fusion, pred[8192]{0:T(1024)(128)(4,1)S(1)} %compare_and_fusion), kind=kOutput, calls=%fused_computation.40 | convolution fusion | flops 94617600 | bytes 2043648 | tf_op jit(solution)/shard_map/dot_general | solution.py:172
  99.3 0.7 copy.82
  100.4 111.3 %all-gather.7.cloned.1.call-done = f32[8192,33]{1,0:T(8,128)} async-done(((f32[32,33]{1,0:T(8,128)}), f32[8192,33]{1,0:T(8,128)}) %all-gather.7.cloned.1.call-update) | async-done | bytes 1081360 | tf_op jit(solution)/shard_map/all_gather | solution.py:42
  211.7 5.3 %slice_bitcast_fusion = f32[3,8192]{0,1:T(8,128)} fusion(f32[8192,33]{1,0:T(8,128)} %all-gather.7.cloned.1.call-done), kind=kLoop, calls=%fused_computation.33 | loop fusion | bytes 196608 | tf_op jit(solution)/shard_map/transpose | solution.py:46
  217.1 2.8 copy.84
  219.9 4.5 %slice_bitcast_fusion.1 = f32[30,8192]{0,1:T(8,128)} fusion(f32[8192,33]{1,0:T(8,128)} %all-gather.7.cloned.1.call-done), kind=kLoop, calls=%fused_computation.34 | loop fusion | bytes 1966080 | tf_op jit(solution)/shard_map/transpose | solution.py:46
  224.4 2.9 copy.83
  227.2 71.6 %while.14 = (s32[]{:T(128)}, f32[30,2048]{1,0:T(8,128)S(1)}, f32[30,8192]{1,0:T(8,128)S(1)}, f32[3,8192]{1,0:T(4,128)S(1)}, f32[3,2048]{1,0:T(4,128)S(1)}, /*ind...) while((s32[]{:T(128)}, f32[30,2048]{1,0:T(8,128)S(1)}, ...), condition=%wide.region_1.2_spmd.clone, body=%wide.region_0.1_spmd.clone.sunk | while | flops 194109440 | bytes 623829 | solution.py:162
  227.4 2.1 convolution_add_fusion.2
  229.6 2.1 convolution_add_fusion.2
  231.8 2.1 convolution_add_fusion.2
  234.1 2.1 convolution_add_fusion.2
  236.3 2.1 convolution_add_fusion.2
  238.5 2.1 convolution_add_fusion.2
  240.8 2.1 convolution_add_fusion.2
  243.0 2.1 convolution_add_fusion.2
  245.3 2.1 convolution_add_fusion.2
  247.5 2.1 convolution_add_fusion.2
  249.7 2.1 convolution_add_fusion.2
  252.0 2.1 convolution_add_fusion.2
  254.2 2.1 convolution_add_fusion.2
  256.5 2.1 convolution_add_fusion.2
  258.7 2.1 convolution_add_fusion.2
  260.9 2.1 convolution_add_fusion.2
  263.2 2.1 convolution_add_fusion.2
  265.4 2.1 convolution_add_fusion.2
  267.6 2.1 convolution_add_fusion.2
  269.9 2.1 convolution_add_fusion.2
  272.1 2.1 convolution_add_fusion.2
  274.4 2.1 convolution_add_fusion.2
  276.6 2.1 convolution_add_fusion.2
  278.8 2.1 convolution_add_fusion.2
  281.1 2.1 convolution_add_fusion.2
  283.3 2.1 convolution_add_fusion.2
  285.5 2.1 convolution_add_fusion.2
  287.8 2.1 convolution_add_fusion.2
  290.0 2.1 convolution_add_fusion.2
  292.3 2.1 convolution_add_fusion.2
  294.5 2.1 convolution_add_fusion.2
  296.7 2.1 convolution_add_fusion.2
  299.3 27.7 %gather_fusion.1 = f32[8192,30]{1,0:T(8,128)} fusion(f32[30,2048]{0,1:T(8,128)S(1)} %copy.85, s32[8192]{0:T(1024)S(1)} %bitcast_clamp_fusion), kind=kCustom, calls=%fused_computation.9 | custom fusion | bytes 1998848 | tf_op jit(solution)/shard_map/jit(_take)/gather | solution.py:96
  327.0 3.2 copy.113
  330.4 0.7 copy-done.3
  331.1 1.4 fusion.28
  332.9 0.8 add_bitcast_fusion
  333.8 0.8 pad_maximum_fusion
  334.9 0.6 gather_fusion.2
  335.7 2.2 collective-permute-start.1
  338.1 0.6 gather_fusion.3
  338.9 3.4 collective-permute-start
  342.5 0.6 gather_fusion.5
  343.3 1.2 collective-permute-start.2
  345.5 3.7 %collective-permute-start.3 = (f32[5,16,32]{1,0,2:T(8,128)S(1)}, f32[5,16,32]{1,0,2:T(8,128)S(1)}, u32[]{:S(2)}, u32[]{:S(2)}) collective-permute-start(f32[5,16,32]{1,0,2:T(8,128)S(1)} %get-tuple-element.172), channel_id=1, source_target_pairs={{0,31},{1,0},{2,1},{3,2},{4,3},{5,4},{6,5},{7,6},{8,7},{9,8},{10,9... | collective-permute-start | bytes 30728 | tf_op jit(solution)/shard_map/ppermute | solution.py:61
  350.6 0.8 collective-permute-done.2
  352.4 0.6 gather_fusion.9
  353.2 0.8 fusion.31
  (145 shorter events, 10.1 us)
Async XLA Ops:
  7.2 82.1 %copy-start = (f32[32,8192]{1,0:T(8,128)S(1)}, f32[32,8192]{1,0:T(8,128)}, u32[]{:S(2)}) copy-start(f32[32,8192]{1,0:T(8,128)} %param.21) | copy-start | bytes 3145732
  7.2 204.5 %all-gather.7.cloned.1.call-start = ((), (), s32[]{:S(2)}) async-start(), calls=%async_computation | async-start | bytes 4210688 | tf_op jit(solution)/shard_map/all_gather | solution.py:42
  89.3 10.0 %copy-start.4 = (f32[3,32]{1,0:T(4,128)S(1)}, f32[3,32]{1,0:T(4,128)}, u32[]{:S(2)}) copy-start(f32[3,32]{1,0:T(4,128)} %param.17) | copy-start | bytes 1156
  89.3 10.8 %copy-start.1 = (f32[3,2048]{1,0:T(4,128)S(1)}, f32[3,2048]{1,0:T(4,128)}, u32[]{:S(2)}) copy-start(f32[3,2048]{1,0:T(4,128)} %param.16) | copy-start | bytes 73732
  89.3 10.9 %copy-start.5 = (s32[1,1,4,32]{3,2,1,0:T(4,128)S(1)}, s32[1,1,4,32]{3,2,1,0:T(4,128)}, u32[]{:S(2)}) copy-start(s32[1,1,4,32]{3,2,1,0:T(4,128)} %param.23) | copy-start | bytes 1540
  89.3 11.0 %copy-start.6 = (s32[1,1,4,32]{3,2,1,0:T(4,128)S(1)}, s32[1,1,4,32]{3,2,1,0:T(4,128)}, u32[]{:S(2)}) copy-start(s32[1,1,4,32]{3,2,1,0:T(4,128)} %param.24) | copy-start | bytes 1540
  89.3 11.0 %copy-start.2 = (s32[64,128]{1,0:T(8,128)S(1)}, s32[64,128]{1,0:T(8,128)}, u32[]{:S(2)}) copy-start(s32[64,128]{1,0:T(8,128)} %param.22) | copy-start | bytes 98308
  330.2 0.8 copy-start.3
  335.7 13.6 %collective-permute-start.1 = (f32[5,16,32]{1,0,2:T(8,128)S(1)}, f32[5,16,32]{1,0,2:T(8,128)S(1)}, u32[]{:S(2)}, u32[]{:S(2)}) collective-permute-start(f32[5,16,32]{1,0,2:T(8,128)S(1)} %get-tuple-element.168), channel_id=1, source_target_pairs={{32,0},{64,32},{96,64},{128,96},{160,128},{192,160},{224,192},{33,... | collective-permute-start | bytes 30728 | tf_op jit(solution)/shard_map/ppermute | solution.py:55
  338.9 11.0 %collective-permute-start = (f32[5,16,32]{1,0,2:T(8,128)S(1)}, f32[5,16,32]{1,0,2:T(8,128)S(1)}, u32[]{:S(2)}, u32[]{:S(2)}) collective-permute-start(f32[5,16,32]{1,0,2:T(8,128)S(1)} %get-tuple-element.170), channel_id=1, source_target_pairs={{0,32},{32,64},{64,96},{96,128},{128,160},{160,192},{192,224},{1,3... | collective-permute-start | bytes 30728 | tf_op jit(solution)/shard_map/ppermute | solution.py:55
  343.3 8.1 %collective-permute-start.2 = (f32[5,16,32]{1,0,2:T(8,128)S(1)}, f32[5,16,32]{1,0,2:T(8,128)S(1)}, u32[]{:S(2)}, u32[]{:S(2)}) collective-permute-start(f32[5,16,32]{1,0,2:T(8,128)S(1)} %get-tuple-element.174), channel_id=1, source_target_pairs={{0,1},{1,2},{2,3},{3,4},{4,5},{5,6},{6,7},{7,8},{8,9},{9,10},{10,1... | collective-permute-start | bytes 30728 | tf_op jit(solution)/shard_map/ppermute | solution.py:61
  345.5 6.9 %collective-permute-start.3 = (f32[5,16,32]{1,0,2:T(8,128)S(1)}, f32[5,16,32]{1,0,2:T(8,128)S(1)}, u32[]{:S(2)}, u32[]{:S(2)}) collective-permute-start(f32[5,16,32]{1,0,2:T(8,128)S(1)} %get-tuple-element.172), channel_id=1, source_target_pairs={{0,31},{1,0},{2,1},{3,2},{4,3},{5,4},{6,5},{7,6},{8,7},{9,8},{10,9... | collective-permute-start | bytes 30728 | tf_op jit(solution)/shard_map/ppermute | solution.py:61
Sparse Core Ops, SparseCore 0:
  100.2 111.5 all-gather.6
where the time goes:
time: 361 us
  waiting for transfers between devices  112 us (31%)
  local copies, waits for them, and re-layouts  88.7 us (25%)
  matrix products  78.6 us (22%)
  blocking collectives  49.8 us (14%)
  between operations  15.3 us (4%)
  starting transfers between devices  10.5 us (3%)
  other arithmetic  4.66 us (1%)
    all_gather x1, waiting for transfers between devices, gather_turned(): whole = lax.all_gather(both, axis, axis=0, tiled=True)  111 us
    dot_general x32, matrix products, step(): jnp.dot(weight_block, kernel, precision=lax.Precision.HIGHEST, preferred_...  67.3 us
    all_gather x3, blocking collectives, stacked_from(): parts = lax.all_gather(parts, axes[k])  42 us
    gather x2, local copies, waits for them, and re-layouts, element_metrics(): jnp.take(jnp.concatenate([moved, node_rows[3 * sections:]], axis=0), link...  30.9 us
    gather x1, local copies, waits for them, and re-layouts, on_device(): right_side = jnp.take(table, every_id, axis=1)  27.7 us
    dot_general x1, matrix products, on_device(): lax.dot_general(right_side, minv, (((1,), (1,)), ((), ())), precision=hig...  9.97 us
    transpose x2, local copies, waits for them, and re-layouts, gather_turned(): jnp.moveaxis(b.reshape(-1, *t.shape[1:]), 0, dim)  9.81 us
    unnamed x20, local copies, waits for them, and re-layouts  8.74 us
  transfers between devices with their start and end apart: 5, of which 2 were waited for; matrix products, arithmetic and copies ran while one was open for 2% of the time, Pallas kernels for 0%

commit v1 on v0

v1 whole, which is shorter than its diff:
```python
import functools

import jax
import jax.numpy as jnp
import numpy as np
from jax import lax
from jax.experimental import pallas as pl
from jax.experimental.pallas import tpu as pltpu
from jax.sharding import Mesh
from jax.sharding import PartitionSpec as P

SPAN_CHORD = ("y", "core", "z", "x")
SPAN = ("y", "core")
CHORD = ("z", "x")
NY, NCORE, NZ, NX = 4, 2, 8, 4
DEVICES = NY * NCORE * NZ * NX
GROUP = NCORE * NZ
MESH = pl.DeviceIdType.MESH
F32 = jnp.float32
BF16 = jnp.bfloat16

WIDTH = 0.1
HALF_INV = 1.0 / (2.0 * WIDTH**2)
CROSS = float(2.0 * HALF_INV * np.log2(np.e))
STORED = 22
TILES = 8


def lobatto_derivative():
    points = np.array([-1.0, -1.0 / np.sqrt(5.0), 1.0 / np.sqrt(5.0), 1.0])
    barycentric = np.array(
        [
            1.0 / np.prod([points[t] - points[s] for s in range(4) if s != t])
            for t in range(4)
        ]
    )
    derivative = np.zeros((4, 4))
    for t in range(4):
        for s in range(4):
            if s != t:
                derivative[t, s] = barycentric[s] / barycentric[t] / (points[t] - points[s])
        derivative[t, t] = -np.sum(derivative[t])
    return derivative


def split3(value):
    high = value.astype(BF16)
    rest = value - high.astype(F32)
    middle = rest.astype(BF16)
    low = (rest - middle.astype(F32)).astype(BF16)
    return high, middle, low


def one_hot(index, blocks):
    width = index.shape[1]
    block = jnp.floor(index * (1.0 / 128.0))
    lane = (index - block * 128.0).astype(BF16)
    block = jnp.broadcast_to(block.astype(BF16), (128, width))
    row = lax.broadcasted_iota(jnp.int32, (128, width), 0).astype(F32).astype(BF16)
    one = jnp.ones((128, width), BF16)
    zero = jnp.zeros((128, width), BF16)
    inner = jnp.where(row == jnp.broadcast_to(lane, (128, width)), one, zero)
    return jnp.concatenate(
        [jnp.where(block == jnp.full((128, width), b, BF16), inner, zero) for b in range(blocks)],
        axis=0,
    )


def kernel(
    ids_ref,
    ctrl_ref,
    nodes_ref,
    shift_ref,
    speed_ref,
    minv_ref,
    conn_ref,
    elem_ref,
    match_ref,
    det_ref,
    flux_ref,
    face_ref,
    own_ref,
    g1_ref,
    g2_ref,
    gp_ref,
    idr_ref,
    table_ref,
    r3_ref,
    m3_ref,
    cross_ref,
    wt_ref,
    scale_ref,
    wc_ref,
    kh_ref,
    kl_ref,
    cb0_ref,
    cb1_ref,
    ns_ref,
    t3_ref,
    gat_ref,
    fl_ref,
    tr_ref,
    rc_ref,
    send1,
    recv1,
    send2,
    recv2,
    send3,
    recv3,
    send4,
    recv4,
    send5,
    recv5,
    send6,
    recv6,
):
    y, core, z, x = (lax.axis_index(name) for name in SPAN_CHORD)
    group = y * NX + x
    place = core * NZ + z
    line = [(dc, dz) for dc in range(NCORE) for dz in range(NZ) if (dc, dz) != (0, 0)]
    plane = [(dy, dx) for dy in range(NY) for dx in range(NX) if (dy, dx) != (0, 0)]

    def line_device(dc, dz):
        return (y, lax.rem(core + dc, NCORE), lax.rem(z + dz, NZ), x)

    def plane_device(dy, dx):
        return (lax.rem(y + dy, NY), core, z, lax.rem(x + dx, NX))

    span = y * NCORE + core
    chord = z * NX + x

    def span_device(step):
        j = lax.rem(span + step + NY * NCORE, NY * NCORE)
        return (j // NCORE, lax.rem(j, NCORE), z, x)

    def chord_device(step):
        k = lax.rem(chord + step + NZ * NX, NZ * NX)
        return (y, core, k // NX, lax.rem(k, NX))

    partner = (y, 1 - core, z, x)
    beside = [span_device(1), span_device(-1), chord_device(1), chord_device(-1)]

    barrier = pltpu.get_barrier_semaphore()
    greeted = [line_device(*d) for d in line] + [plane_device(*d) for d in plane] + beside
    for device in greeted:
        pl.semaphore_signal(barrier, inc=1, device_id=device, device_id_type=MESH)

    own_ref[0] = jnp.concatenate(
        [ids_ref[...].astype(F32)] + [ctrl_ref[k : k + 1, :] for k in range(3)], axis=1
    )
    g1_ref[group * GROUP + place] = own_ref[0]
    table = jnp.concatenate(
        [shift_ref[...], speed_ref[...], jnp.zeros((2, shift_ref.shape[1]), F32)], axis=0
    )
    for k, part in enumerate(split3(table)):
        table_ref[k * 32 : (k + 1) * 32, :] = part

    pl.semaphore_wait(barrier, len(greeted))

    def first_copy(k, device):
        return pltpu.make_async_remote_copy(
            src_ref=own_ref,
            dst_ref=g1_ref.at[pl.ds(group * GROUP + place, 1)],
            send_sem=send1.at[k],
            recv_sem=recv1.at[k],
            device_id=device,
            device_id_type=MESH,
        )

    copies1 = [first_copy(k, line_device(*d)) for k, d in enumerate(line)]
    for copy in copies1:
        copy.start()
    for k, part in enumerate(split3(minv_ref[...])):
        m3_ref[k * 32 : (k + 1) * 32, :] = part
    ns_ref[...] = nodes_ref[...] * CROSS
    for copy in copies1:
        copy.wait_recv()

    def second_copy(k, device):
        rows = pl.ds(group * GROUP, GROUP)
        return pltpu.make_async_remote_copy(
            src_ref=g1_ref.at[rows],
            dst_ref=g1_ref.at[rows],
            send_sem=send2.at[k],
            recv_sem=recv2.at[k],
            device_id=device,
            device_id_type=MESH,
        )

    copies2 = [second_copy(k, plane_device(*d)) for k, d in enumerate(plane)]
    for copy in copies2:
        copy.start()
    for copy in copies1:
        copy.wait_send()
    for copy in copies2:
        copy.wait_recv()
    for copy in copies2:
        copy.wait_send()

    gp_ref[...] = g1_ref[...].reshape(DEVICES, 128)
    for ny in range(NY):
        idr_ref[ny * GROUP : (ny + 1) * GROUP, :] = jnp.concatenate(
            [gp_ref[(ny * NX + q) * GROUP : (ny * NX + q + 1) * GROUP, 0:32] for q in range(NX)],
            axis=1,
        )

    def selected(accs, parts_ref, index, blocks, which):
        spread = one_hot(index, blocks)
        for k in range(blocks // 2):
            pltpu.matmul_push_rhs(
                spread[k * 256 : (k + 1) * 256], staging_register=0, mxu_index=which % 2
            )
            pltpu.matmul_acc_lhs(
                accs[which], parts_ref[:, k * 256 : (k + 1) * 256], load_staged_rhs=0
            )

    def first_stage(*accs):
        for acc in accs:
            pltpu.matmul_pop(acc)

        def right_side(i, carry):
            for u in range(8):
                pair = idr_ref[pl.ds((i * 8 + u) * 2, 2), :]
                index = jnp.concatenate([pair[0:1], pair[1:2]], axis=1)
                selected(accs, table_ref, index, 8, u)
            for u in range(8):
                lanes = pl.ds(pl.multiple_of((i * 8 + u) * 256, 256), 256)
                r3_ref[:, lanes] = pltpu.matmul_pop(accs[u]).astype(BF16)
            return carry

        lax.fori_loop(0, 4, right_side, 0)

        for k in range(32):
            lanes = slice(k * 256, (k + 1) * 256)
            pltpu.matmul_push_rhs(
                jnp.concatenate([r3_ref[:, lanes], jnp.zeros((160, 256), BF16)], axis=0),
                staging_register=0,
                mxu_index=k % 2,
                transpose=True,
            )
            pltpu.matmul_acc_lhs(accs[k % 2], m3_ref[:, lanes], load_staged_rhs=0)
        cross_ref[...] = pltpu.matmul_pop(accs[0]) + pltpu.matmul_pop(accs[1])

    pl.run_scoped(first_stage, *[pltpu.ACC(u % 2)((96, 256), F32) for u in range(8)])
    cross = cross_ref[...]

    def piece(a, b):
        return cross[a * 32 : (a + 1) * 32, b * 32 : (b + 1) * 32]

    weights = piece(0, 0) + (
        (piece(0, 1) + piece(1, 0)) + (piece(1, 1) + (piece(0, 2) + piece(2, 0)))
    )
    wt_ref[:, 0:32] = weights
    mine = group * GROUP + place
    g2_ref[mine] = jnp.concatenate(
        [wt_ref[pl.ds(q, 8, stride=4), 0:32] for q in range(4)], axis=1
    )

    def third_copy(k, device):
        return pltpu.make_async_remote_copy(
            src_ref=g2_ref.at[pl.ds(mine, 1)],
            dst_ref=g2_ref.at[pl.ds(mine, 1)],
            send_sem=send3.at[k],
            recv_sem=recv3.at[k],
            device_id=device,
            device_id_type=MESH,
        )

    copies3 = [third_copy(k, line_device(0, k + 1)) for k in range(NZ - 1)]
    for copy in copies3:
        copy.start()

    def columns(l, target):
        for k in range(3):
            column = jnp.full((DEVICES, 128), 32 * (k + 1), jnp.int32) + l
            target[k] = jnp.take_along_axis(
                gp_ref[...], column, axis=1, mode="promise_in_bounds"
            )

    def tile(source, start):
        highs, lows = [], []
        for h in range(2):
            lanes = pl.ds(start + h * 128, 128)
            power = (
                source[0] * ns_ref[0:1, lanes]
                + source[1] * ns_ref[1:2, lanes]
                + source[2] * ns_ref[2:3, lanes]
            )
            value = jnp.exp2(power)
            high = value.astype(BF16)
            highs.append(high)
            lows.append((value - high.astype(F32)).astype(BF16))
        return jnp.concatenate(highs, axis=1), jnp.concatenate(lows, axis=1)

    def generate(l, source):
        def step(i, carry):
            for u in range(2):
                t = i * 2 + u
                high, low = tile(source, pl.multiple_of(t * 256, 256))
                kh_ref[l, t] = high
                kl_ref[l, t] = low
            return carry

        lax.fori_loop(0, TILES // 2, step, 0)

    def generate_range(first, last):
        def step(i, carry):
            l = i * 2
            columns(l, cb0_ref)
            generate(l, cb0_ref)
            columns(l + 1, cb1_ref)
            generate(l + 1, cb1_ref)
            return carry

        lax.fori_loop(first // 2, last // 2, step, 0)

    generate_range(0, 6)
    for copy in copies3:
        copy.wait_recv()

    def block_rows(of_y, of_x, of_core):
        return pl.ds((of_y * NX + of_x) * GROUP + of_core * NZ, NZ)

    def fourth_copy(k, device):
        rows = block_rows(y, x, core)
        return pltpu.make_async_remote_copy(
            src_ref=g2_ref.at[rows],
            dst_ref=g2_ref.at[rows],
            send_sem=send4.at[k],
            recv_sem=recv4.at[k],
            device_id=device,
            device_id_type=MESH,
        )

    copies4 = [fourth_copy(k, plane_device(*d)) for k, d in enumerate(plane)]
    for copy in copies4:
        copy.start()

    def fifth_copy(k, dy, dx):
        rows = block_rows(lax.rem(y + NY - dy, NY), lax.rem(x + NX - dx, NX), core)
        return pltpu.make_async_remote_copy(
            src_ref=g2_ref.at[rows],
            dst_ref=g2_ref.at[rows],
            send_sem=send5.at[k],
            recv_sem=recv5.at[k],
            device_id=partner,
            device_id_type=MESH,
        )

    copies5 = [fifth_copy(k, *d) for k, d in enumerate([(0, 0)] + plane)]
    copies5[0].start()
    for copy in copies3:
        copy.wait_send()
    generate_range(6, 16)
    for k in range(len(plane)):
        copies4[k].wait_recv()
        copies5[k + 1].start()
    for copy in copies4:
        copy.wait_send()
    turned = gp_ref[...].T
    scale_ref[...] = jnp.exp(
        -HALF_INV * (turned[32:64] ** 2 + turned[64:96] ** 2 + turned[96:128] ** 2)
    )
    generate_range(16, STORED)
    for copy in copies5:
        copy.wait_recv()
    for copy in copies5:
        copy.wait_send()

    for j in range(8):
        block = g2_ref[:, j, :].T
        for q in range(4):
            l = 4 * j + q
            value = block[q * 32 : (q + 1) * 32] * scale_ref[l : l + 1, :]
            high = value.astype(BF16)
            wc_ref[l, 0:32, :] = high
            wc_ref[l, 32:64, :] = (value - high.astype(F32)).astype(BF16)

    def products(highs, lows):
        for a, b in zip(highs, lows):
            pltpu.matmul_pop(a)
            pltpu.matmul_pop(b)

        def add(l, t, high, low):
            pltpu.matmul_push_rhs(high, staging_register=0, mxu_index=0)
            pltpu.matmul_acc_lhs(highs[t], wc_ref[l], load_staged_rhs=0)
            pltpu.matmul_push_rhs(low, staging_register=0, mxu_index=1)
            pltpu.matmul_acc_lhs(lows[t], wc_ref[l, 0:32], load_staged_rhs=0)

        def stored(l, carry):
            for t in range(TILES):
                add(l, t, kh_ref[l, t], kl_ref[l, t])
            return carry

        lax.fori_loop(0, STORED, stored, 0)

        def fresh(i, carry):
            for u, buffer in enumerate((cb0_ref, cb1_ref)):
                l = i * 2 + u
                columns(l, buffer)
                for t in range(TILES):
                    add(l, t, *tile(buffer, t * 256))
            return carry

        lax.fori_loop(STORED // 2, 16, fresh, 0)
        for t in range(TILES):
            lanes = slice(t * 256, (t + 1) * 256)
            first = pltpu.matmul_pop(highs[t])
            total = first[0:32] + first[32:64] + pltpu.matmul_pop(lows[t])
            place_of = nodes_ref[:, lanes]
            factor = jnp.exp(-HALF_INV * jnp.sum(place_of * place_of, axis=0, keepdims=True))
            base = jnp.concatenate([place_of] * 5 + [jnp.zeros((17, 256), F32)], axis=0)
            for k, part in enumerate(split3(total * factor + base)):
                t3_ref[k * 32 : (k + 1) * 32, lanes] = part

    pl.run_scoped(
        products,
        tuple(pltpu.ACC(0)((64, 256), F32) for _ in range(TILES)),
        tuple(pltpu.ACC(1)((32, 256), F32) for _ in range(TILES)),
    )

    def last_stage(*accs):
        for acc in accs:
            pltpu.matmul_pop(acc)

        def gather(i, carry):
            for u in range(8):
                pair = conn_ref[pl.ds((i * 8 + u) * 2, 2), :].astype(F32)
                index = jnp.concatenate([pair[0:1], pair[1:2]], axis=1)
                selected(accs, t3_ref, index, 16, u)
            for u in range(8):
                parts = pltpu.matmul_pop(accs[u])
                value = parts[0:32] + parts[32:64] + parts[64:96]
                first = (i * 8 + u) * 64
                gat_ref[pl.ds(first, 32), :] = value[:, 0:128]
                gat_ref[pl.ds(first + 32, 32), :] = value[:, 128:256]
            return carry

        lax.fori_loop(0, 4, gather, 0)

    pl.run_scoped(last_stage, *[pltpu.ACC(u % 2)((96, 256), F32) for u in range(8)])

    derivative = lobatto_derivative()

    def rows(first, p):
        return gat_ref[pl.ds(p * 32 + first, 5, stride=3), :]

    def metrics(p):
        a, b, c = p // 16, (p // 4) % 4, p % 4
        lines = (
            (a, [k * 16 + b * 4 + c for k in range(4)]),
            (b, [a * 16 + k * 4 + c for k in range(4)]),
            (c, [a * 16 + b * 4 + k for k in range(4)]),
        )
        jac = [[None] * 3 for _ in range(3)]
        for i in range(3):
            for d, (at, points) in enumerate(lines):
                terms = [
                    float(derivative[at, k]) * rows(i, q)
                    for k, q in enumerate(points)
                    if derivative[at, k] != 0.0
                ]
                jac[i][d] = functools.reduce(jnp.add, terms)

        def metric(d, i):
            i1, i2, d1, d2 = (i + 1) % 3, (i + 2) % 3, (d + 1) % 3, (d + 2) % 3
            return jac[i1][d1] * jac[i2][d2] - jac[i1][d2] * jac[i2][d1]

        speed = [rows(15 + i, p) for i in range(3)]
        entries = [[metric(d, i) for i in range(3)] for d in range(3)]
        det = (
            jac[0][0] * entries[0][0] + jac[0][1] * entries[1][0] + jac[0][2] * entries[2][0]
        )
        det_ref[:, p, :] = det
        for d in range(3):
            value = (
                entries[d][0] * speed[0] + entries[d][1] * speed[1] + entries[d][2] * speed[2]
            )
            flux_ref[:, d, p, :] = value
            if d > 0:
                fl_ref[d - 1, p, 0:5, :] = value

    fl_ref[...] = jnp.zeros_like(fl_ref)
    for p in range(64):
        metrics(p)

    lane = lax.broadcasted_iota(jnp.int32, (8, 128), 1)

    def quarters(values):
        out = values[0]
        for q in range(1, 4):
            out = jnp.where(lane >= q * 32, values[q], out)
        return out

    for t in range(4):
        index = jnp.broadcast_to(
            jnp.concatenate([elem_ref[t : t + 1, :]] * 4, axis=1), (8, 128)
        )
        for a in range(4):
            if t < 2:
                points = [a * 16 + q * 4 + 3 * t for q in range(4)]
            else:
                points = [a * 16 + 12 * (t - 2) + q for q in range(4)]
            picked = quarters(
                [
                    jnp.take_along_axis(
                        fl_ref[1 - t // 2, p], index, axis=1, mode="promise_in_bounds"
                    )
                    for p in points
                ]
            )
            tr_ref[t, a] = picked if t % 2 else -picked

    across = [(0, beside[1], 1), (1, beside[0], 0), (2, beside[3], 3), (3, beside[2], 2)]
    copies6 = [
        pltpu.make_async_remote_copy(
            src_ref=tr_ref.at[t],
            dst_ref=rc_ref.at[slot],
            send_sem=send6.at[t],
            recv_sem=recv6.at[slot],
            device_id=device,
            device_id_type=MESH,
        )
        for t, device, slot in across
    ]
    for copy in copies6:
        copy.start()
    for copy in copies6:
        copy.wait_recv()
    for copy in copies6:
        copy.wait_send()

    for t in range(4):
        index = jnp.broadcast_to(
            jnp.concatenate([match_ref[t : t + 1, :] + 32 * q for q in range(4)], axis=1), (8, 128)
        )
        for a in range(4):
            own = tr_ref[t, a]
            other = jnp.take_along_axis(rc_ref[t, a], index, axis=1, mode="promise_in_bounds")
            if t == 0:
                other = jnp.where(jnp.broadcast_to(span == 0, (8, 128)), -own, other)
            if t == 1:
                other = jnp.where(
                    jnp.broadcast_to(span == NY * NCORE - 1, (8, 128)), -own, other
                )
            value = 0.5 * (own - other)
            for q in range(4):
                face_ref[t, :, a * 4 + q, :] = value[0:5, q * 32 : (q + 1) * 32]


def on_device(
    node_pos, ctrl_pos, ctrl_ids, wing_shift, wing_speed, minv, conn, face_elem, face_match
):
    vmem = pl.BlockSpec(memory_space=pltpu.VMEM)
    dma = pltpu.SemaphoreType.DMA
    det, flux, face = pl.pallas_call(
        kernel,
        out_shape=(
            jax.ShapeDtypeStruct((5, 64, 128), F32),
            jax.ShapeDtypeStruct((5, 3, 64, 128), F32),
            jax.ShapeDtypeStruct((4, 5, 16, 32), F32),
        ),
        in_specs=[vmem] * 9,
        out_specs=[vmem] * 3,
        scratch_shapes=[
            pltpu.VMEM((1, 1, 128), F32),
            pltpu.VMEM((DEVICES, 1, 128), F32),
            pltpu.VMEM((DEVICES, 8, 128), F32),
            pltpu.VMEM((DEVICES, 128), F32),
            pltpu.VMEM((64, 128), F32),
            pltpu.VMEM((96, 1024), BF16),
            pltpu.VMEM((96, 8192), BF16),
            pltpu.VMEM((96, 8192), BF16),
            pltpu.VMEM((96, 256), F32),
            pltpu.VMEM((32, 128), F32),
            pltpu.VMEM((32, DEVICES), F32),
            pltpu.VMEM((32, 64, DEVICES), BF16),
            pltpu.VMEM((STORED, TILES, 256, 256), BF16),
            pltpu.VMEM((STORED, TILES, 256, 256), BF16),
            pltpu.VMEM((3, DEVICES, 128), F32),
            pltpu.VMEM((3, DEVICES, 128), F32),
            pltpu.VMEM((3, 2048), F32),
            pltpu.VMEM((96, 2048), BF16),
            pltpu.VMEM((64 * 32, 128), F32),
            pltpu.VMEM((2, 64, 8, 128), F32),
            pltpu.VMEM((4, 4, 8, 128), F32),
            pltpu.VMEM((4, 4, 8, 128), F32),
            dma((15,)),
            dma((15,)),
            dma((15,)),
            dma((15,)),
            dma((7,)),
            dma((7,)),
            dma((15,)),
            dma((15,)),
            dma((16,)),
            dma((16,)),
            dma((4,)),
            dma((4,)),
        ],
        compiler_params=pltpu.CompilerParams(
            collective_id=0, has_side_effects=True, vmem_limit_bytes=66 * 1000 * 1000
        ),
        name="wing",
    )(
        ctrl_ids.reshape(1, 32),
        ctrl_pos,
        node_pos,
        wing_shift,
        wing_speed,
        minv,
        conn,
        face_elem.reshape(4, 32),
        face_match.reshape(4, 32),
    )
    return det, flux, face.reshape(1, 1, 4, 5, 16, 32)


def solution(mesh):
    split = Mesh(mesh.devices.reshape(NY, NCORE, NZ, NX), SPAN_CHORD)
    return jax.shard_map(
        on_device,
        mesh=split,
        in_specs=(
            P(None, SPAN_CHORD),
            P(None, SPAN_CHORD),
            P(SPAN_CHORD),
            P(),
            P(),
            P(SPAN_CHORD, None),
            P(None, SPAN_CHORD),
            P(SPAN, CHORD, None, None),
            P(SPAN, CHORD, None, None),
        ),
        out_specs=(
            P(None, None, SPAN_CHORD),
            P(None, None, None, SPAN_CHORD),
            P(SPAN, CHORD, None, None, None, None),
        ),
        check_vma=False,
    )
```

time: 361 us -> 80.6 us (0.22)
  waiting for transfers between devices: 112 us -> 0 us
  local copies, waits for them, and re-layouts: 88.7 us -> 4.15 us
  matrix products: 78.6 us -> 0 us
  Pallas kernels: 0 us -> 75.6 us
  blocking collectives: 49.8 us -> 0 us
  between operations: 15.3 us -> 0.64 us
  starting transfers between devices: 10.5 us -> 0 us
  other arithmetic: 4.66 us -> 0 us
    all_gather x1 -> x0, waiting for transfers between devices: 111 us -> none  [gather_turned(): whole = lax.all_gather(both, axis, axis=0, tiled=True)]
    dot_general x34 -> x0, matrix products: 78.6 us -> none  [the longest x32 67.3 us: step(): jnp.dot(weight_block, kernel, precision=lax.Precision.HIGHEST, preferred_...]
    pallas_call x0 -> x1, Pallas kernels: none -> 75.6 us  [on_device(): pl.pallas_call(kernel, out_shape=(jax.ShapeDtypeStruct((5, 64, 128), F32)...]
    gather x11 -> x0, local copies, waits for them, and re-layouts: 63.3 us -> none  [the longest x2 30.9 us: element_metrics(): jnp.take(jnp.concatenate([moved, node_rows[3 * sections:]], axis=0), link...]
    all_gather x3 -> x0, blocking collectives: 42 us -> none  [stacked_from(): parts = lax.all_gather(parts, axes[k])]
    ppermute x4 -> x0, starting transfers between devices: 10.4 us -> none  [the longest x2 5.56 us: passed_along(): return lax.ppermute(block, axis, route)]
    transpose x3 -> x0, local copies, waits for them, and re-layouts: 9.89 us -> none  [the longest x2 9.81 us: gather_turned(): jnp.moveaxis(b.reshape(-1, *t.shape[1:]), 0, dim)]
    unnamed x1 -> x0, blocking collectives: 7.85 us -> none
  transfers between devices with their start and end apart: 5 -> 0, of which waited for: 2 -> 0; matrix products, arithmetic and copies ran while one was open for 2% -> 0% of each run, Pallas kernels for 0% -> 0%
where the time goes in v1:
time: 80.6 us; the launch traced here: 80.4 us
  Pallas kernels  75.6 us (94%)
  local copies, waits for them, and re-layouts  4.15 us (5%)
    pallas_call x1, Pallas kernels, on_device(): pl.pallas_call(kernel, out_shape=(jax.ShapeDtypeStruct((5, 64, 128), F32)...  75.6 us
    unnamed x5, local copies, waits for them, and re-layouts  4.15 us

profile of v1, /device:TPU:1, one launch (start us, length us, event | category | flops | bytes accessed | tf_op | source)
XLA Modules:
  0.0 80.4 jit_solution(1272480392681688961)
XLA Ops:
  0.6 75.6 %wing.1 = (f32[5,64,128]{2,1,0:T(8,128)}, f32[5,3,64,128]{3,2,1,0:T(8,128)}, f32[4,5,16,32]{3,2,1,0:T(8,128)}) custom-call(s32[1,32]{1,0:T(1,128)} %bitcast.7, f32[3,32]{1,0:T(4,128)} %ctrl_ref.1, f32[3,2048]{1,0:T(4,128)} %nodes_ref.1, f32[15,1024]{1,0:T(8,128)} %shift_ref.1, f32[15,1024]{1,0:T(8,128)} %speed_ref.1, f32[32,8192]{1,0:T(8,128)} %minv_ref.1, ...), custom_call_target="tpu_custom_call" | custom-call | tf_op jit(solution)/shard_map/wing/pallas_call | solution.py:556
  76.2 1.6 %copy.15 = f32[5,64,128]{2,1,0:T(8,128)} copy(f32[5,64,128]{2,1,0:T(8,128)} %get-tuple-element.12) | data formatting | bytes 327680
  77.8 0.0 copy-start
  77.8 1.9 %copy.16 = f32[5,3,64,128]{3,2,1,0:T(8,128)} copy(f32[5,3,64,128]{3,2,1,0:T(8,128)} %get-tuple-element.13) | data formatting | bytes 983040
  79.7 0.0 copy-done
  79.7 0.7 copy.17
Async XLA Ops:
  77.8 1.9 %copy-start = (f32[4,5,16,32]{3,2,1,0:T(8,128)S(1)}, f32[4,5,16,32]{3,2,1,0:T(8,128)}, u32[]{:S(2)}) copy-start(f32[4,5,16,32]{3,2,1,0:T(8,128)} %get-tuple-element.8) | copy-start | bytes 122884

commit v2 on v1

--- a/solution.py
+++ b/solution.py
@@ -22,8 +22,21 @@
 WIDTH = 0.1
 HALF_INV = 1.0 / (2.0 * WIDTH**2)
 CROSS = float(2.0 * HALF_INV * np.log2(np.e))
-STORED = 22
+STORED = 24
 TILES = 8
+
+
+PAIRS = ((0, 0), (0, 1), (0, 2), (1, 0), (1, 1), (2, 0))
+
+
+def selection():
+    chosen = np.zeros((4, 512, 256), np.float32)
+    for g in range(4):
+        for l in range(8):
+            for j, (part, _) in enumerate(PAIRS):
+                for k in range(3):
+                    chosen[g, part * 128 + 32 * (k + 1) + 8 * g + l, l * 32 + 3 * j + k] = 1.0
+    return jnp.asarray(chosen, BF16)
 
 
 def lobatto_derivative():
@@ -67,6 +80,19 @@
 
 
 def kernel(
+    ids_in,
+    ctrl_in,
+    nodes_in,
+    shift_in,
+    speed_in,
+    minv_in,
+    conn_in,
+    elem_in,
+    match_in,
+    sel_in,
+    det_out,
+    flux_out,
+    face_ref,
     ids_ref,
     ctrl_ref,
     nodes_ref,
@@ -76,9 +102,9 @@
     conn_ref,
     elem_ref,
     match_ref,
+    sel_ref,
     det_ref,
     flux_ref,
-    face_ref,
     own_ref,
     g1_ref,
     g2_ref,
@@ -93,9 +119,9 @@
     wc_ref,
     kh_ref,
     kl_ref,
-    cb0_ref,
-    cb1_ref,
-    ns_ref,
+    parts_ref,
+    lhs_ref,
+    nb_ref,
     t3_ref,
     gat_ref,
     fl_ref,
@@ -113,6 +139,8 @@
     recv5,
     send6,
     recv6,
+    load,
+    store,
 ):
     y, core, z, x = (lax.axis_index(name) for name in SPAN_CHORD)
     group = y * NX + x
@@ -145,6 +173,27 @@
     for device in greeted:
         pl.semaphore_signal(barrier, inc=1, device_id=device, device_id_type=MESH)
 
+    loads = [
+        pltpu.make_async_copy(source, target, load.at[k])
+        for k, (source, target) in enumerate(
+            (
+                (ids_in, ids_ref),
+                (ctrl_in, ctrl_ref),
+                (shift_in, shift_ref),
+                (speed_in, speed_ref),
+                (minv_in, minv_ref),
+                (nodes_in, nodes_ref),
+                (conn_in, conn_ref),
+                (elem_in, elem_ref),
+                (match_in, match_ref),
+                (sel_in, sel_ref),
+            )
+        )
+    ]
+    for copy in loads:
+        copy.start()
+    for copy in loads[:4]:
+        copy.wait()
     own_ref[0] = jnp.concatenate(
         [ids_ref[...].astype(F32)] + [ctrl_ref[k : k + 1, :] for k in range(3)], axis=1
     )
@@ -170,9 +219,14 @@
     copies1 = [first_copy(k, line_device(*d)) for k, d in enumerate(line)]
     for copy in copies1:
         copy.start()
+    for copy in loads[4:]:
+        copy.wait()
     for k, part in enumerate(split3(minv_ref[...])):
         m3_ref[k * 32 : (k + 1) * 32, :] = part
-    ns_ref[...] = nodes_ref[...] * CROSS
+    node_parts = split3(nodes_ref[...] * CROSS)
+    nb_ref[...] = jnp.concatenate(
+        [node_parts[part].astype(F32) for _, part in PAIRS] + [jnp.zeros((14, 2048), F32)], axis=0
+    ).astype(BF16)
     for copy in copies1:
         copy.wait_recv()
 
@@ -270,51 +324,66 @@
     for copy in copies3:
         copy.start()
 
-    def columns(l, target):
-        for k in range(3):
-            column = jnp.full((DEVICES, 128), 32 * (k + 1), jnp.int32) + l
-            target[k] = jnp.take_along_axis(
-                gp_ref[...], column, axis=1, mode="promise_in_bounds"
-            )
-
-    def tile(source, start):
-        highs, lows = [], []
-        for h in range(2):
-            lanes = pl.ds(start + h * 128, 128)
-            power = (
-                source[0] * ns_ref[0:1, lanes]
-                + source[1] * ns_ref[1:2, lanes]
-                + source[2] * ns_ref[2:3, lanes]
-            )
-            value = jnp.exp2(power)
-            high = value.astype(BF16)
-            highs.append(high)
-            lows.append((value - high.astype(F32)).astype(BF16))
-        return jnp.concatenate(highs, axis=1), jnp.concatenate(lows, axis=1)
-
-    def generate(l, source):
-        def step(i, carry):
-            for u in range(2):
-                t = i * 2 + u
-                high, low = tile(source, pl.multiple_of(t * 256, 256))
-                kh_ref[l, t] = high
-                kl_ref[l, t] = low
+    def weights_of(power):
+        value = jnp.exp2(power)
+        high = value.astype(BF16)
+        return high, (value - high.astype(F32)).astype(BF16)
+
+    def cross_rhs(l, lanes):
+        pieces = [nb_ref[:, lanes]]
+        if l > 0:
+            pieces = [jnp.zeros((32 * l, 256), BF16)] + pieces
+        if l < 7:
+            pieces = pieces + [jnp.zeros((32 * (7 - l), 256), BF16)]
+        return jnp.concatenate(pieces, axis=0)
+
+    def generate(accs):
+        def step(t, carry):
+            lanes = pl.ds(pl.multiple_of(t * 256, 256), 256)
+            for l in range(8):
+                pltpu.matmul_push_rhs(cross_rhs(l, lanes), staging_register=0, mxu_index=l % 2)
+                for g in range(3):
+                    pltpu.matmul_acc_lhs(
+                        accs[l % 2][g], lhs_ref[g], load_staged_rhs=0 if g == 0 else None
+                    )
+                for g in range(3):
+                    high, low = weights_of(pltpu.matmul_pop(accs[l % 2][g]))
+                    kh_ref[g * 8 + l, t] = high
+                    kl_ref[g * 8 + l, t] = low
             return carry
 
-        lax.fori_loop(0, TILES // 2, step, 0)
+        return step
+
+    def start_generation(*accs):
+        for acc in accs:
+            pltpu.matmul_pop(acc)
+        for g in range(4):
+            for k in range(2):
+                pltpu.matmul_push_rhs(
+                    sel_ref[g, k * 256 : (k + 1) * 256, :], staging_register=0, mxu_index=g % 2
+                )
+                pltpu.matmul_acc_lhs(accs[g], parts_ref[k], load_staged_rhs=0)
+        for g in range(4):
+            lhs_ref[g] = pltpu.matmul_pop(accs[g]).astype(BF16)
 
     def generate_range(first, last):
-        def step(i, carry):
-            l = i * 2
-            columns(l, cb0_ref)
-            generate(l, cb0_ref)
-            columns(l + 1, cb1_ref)
-            generate(l + 1, cb1_ref)
-            return carry
-
-        lax.fori_loop(first // 2, last // 2, step, 0)
-
-    generate_range(0, 6)
+        def scoped(zero, one):
+            for acc in (*zero, *one):
+                pltpu.matmul_pop(acc)
+            lax.fori_loop(first, last, generate((zero, one)), 0)
+
+        pl.run_scoped(
+            scoped,
+            tuple(pltpu.ACC(0)((256, 256), F32) for _ in range(3)),
+            tuple(pltpu.ACC(1)((256, 256), F32) for _ in range(3)),
+        )
+
+    for k, part in enumerate(split3(gp_ref[...])):
+        parts_ref[k // 2, :, (k % 2) * 128 : (k % 2 + 1) * 128] = part
+    parts_ref[1, :, 128:256] = jnp.zeros((DEVICES, 128), BF16)
+    pl.run_scoped(start_generation, *[pltpu.ACC(g % 2)((256, 256), F32) for g in range(4)])
+
+    generate_range(0, 3)
     for copy in copies3:
         copy.wait_recv()
 
@@ -351,7 +420,7 @@
     copies5[0].start()
     for copy in copies3:
         copy.wait_send()
-    generate_range(6, 16)
+    generate_range(3, 8)
     for k in range(len(plane)):
         copies4[k].wait_recv()
         copies5[k + 1].start()
@@ -361,7 +430,6 @@
     scale_ref[...] = jnp.exp(
         -HALF_INV * (turned[32:64] ** 2 + turned[64:96] ** 2 + turned[96:128] ** 2)
     )
-    generate_range(16, STORED)
     for copy in copies5:
         copy.wait_recv()
     for copy in copies5:
@@ -376,47 +444,50 @@
             wc_ref[l, 0:32, :] = high
             wc_ref[l, 32:64, :] = (value - high.astype(F32)).astype(BF16)
 
-    def products(highs, lows):
-        for a, b in zip(highs, lows):
-            pltpu.matmul_pop(a)
-            pltpu.matmul_pop(b)
-
-        def add(l, t, high, low):
+    def products(zero, one, high_acc, low_acc):
+        accs = (zero, one)
+        for acc in (*zero, *one, high_acc, low_acc):
+            pltpu.matmul_pop(acc)
+
+        def add(l, high, low):
             pltpu.matmul_push_rhs(high, staging_register=0, mxu_index=0)
-            pltpu.matmul_acc_lhs(highs[t], wc_ref[l], load_staged_rhs=0)
+            pltpu.matmul_acc_lhs(high_acc, wc_ref[l], load_staged_rhs=0)
             pltpu.matmul_push_rhs(low, staging_register=0, mxu_index=1)
-            pltpu.matmul_acc_lhs(lows[t], wc_ref[l, 0:32], load_staged_rhs=0)
-
-        def stored(l, carry):
-            for t in range(TILES):
-                add(l, t, kh_ref[l, t], kl_ref[l, t])
-            return carry
-
-        lax.fori_loop(0, STORED, stored, 0)
-
-        def fresh(i, carry):
-            for u, buffer in enumerate((cb0_ref, cb1_ref)):
-                l = i * 2 + u
-                columns(l, buffer)
-                for t in range(TILES):
-                    add(l, t, *tile(buffer, t * 256))
-            return carry
-
-        lax.fori_loop(STORED // 2, 16, fresh, 0)
-        for t in range(TILES):
-            lanes = slice(t * 256, (t + 1) * 256)
-            first = pltpu.matmul_pop(highs[t])
-            total = first[0:32] + first[32:64] + pltpu.matmul_pop(lows[t])
+            pltpu.matmul_acc_lhs(low_acc, wc_ref[l, 0:32], load_staged_rhs=0)
+
+        def columns(t, carry):
+            lanes = pl.ds(pl.multiple_of(t * 256, 256), 256)
+
+            def power(l):
+                pltpu.matmul_push_rhs(cross_rhs(l, lanes), staging_register=1, mxu_index=l % 2)
+                pltpu.matmul_acc_lhs(accs[l % 2][(l // 2) % 2], lhs_ref[3], load_staged_rhs=1)
+
+            power(0)
+            power(1)
+            for l in range(8):
+                high, low = weights_of(pltpu.matmul_pop(accs[l % 2][(l // 2) % 2]))
+                if l < 6:
+                    power(l + 2)
+                for k in range(3 * l, 3 * l + 3):
+                    add(k, kh_ref[k, t], kl_ref[k, t])
+                add(24 + l, high, low)
+            first = pltpu.matmul_pop(high_acc)
+            total = first[0:32] + first[32:64] + pltpu.matmul_pop(low_acc)
             place_of = nodes_ref[:, lanes]
             factor = jnp.exp(-HALF_INV * jnp.sum(place_of * place_of, axis=0, keepdims=True))
             base = jnp.concatenate([place_of] * 5 + [jnp.zeros((17, 256), F32)], axis=0)
             for k, part in enumerate(split3(total * factor + base)):
                 t3_ref[k * 32 : (k + 1) * 32, lanes] = part
+            return carry
+
+        lax.fori_loop(0, TILES, columns, 0)
 
     pl.run_scoped(
         products,
-        tuple(pltpu.ACC(0)((64, 256), F32) for _ in range(TILES)),
-        tuple(pltpu.ACC(1)((32, 256), F32) for _ in range(TILES)),
+        tuple(pltpu.ACC(0)((256, 256), F32) for _ in range(2)),
+        tuple(pltpu.ACC(1)((256, 256), F32) for _ in range(2)),
+        pltpu.ACC(0)((64, 256), F32),
+        pltpu.ACC(1)((32, 256), F32),
     )
 
     def last_stage(*accs):
@@ -445,7 +516,7 @@
     def rows(first, p):
         return gat_ref[pl.ds(p * 32 + first, 5, stride=3), :]
 
-    def metrics(p):
+    def jacobian(p, directions):
         a, b, c = p // 16, (p // 4) % 4, p % 4
         lines = (
             (a, [k * 16 + b * 4 + c for k in range(4)]),
@@ -454,35 +525,44 @@
         )
         jac = [[None] * 3 for _ in range(3)]
         for i in range(3):
-            for d, (at, points) in enumerate(lines):
+            for d in directions:
+                at, points = lines[d]
                 terms = [
                     float(derivative[at, k]) * rows(i, q)
                     for k, q in enumerate(points)
                     if derivative[at, k] != 0.0
                 ]
                 jac[i][d] = functools.reduce(jnp.add, terms)
-
-        def metric(d, i):
-            i1, i2, d1, d2 = (i + 1) % 3, (i + 2) % 3, (d + 1) % 3, (d + 2) % 3
-            return jac[i1][d1] * jac[i2][d2] - jac[i1][d2] * jac[i2][d1]
-
+        return jac
+
+    def metric(jac, d, i):
+        i1, i2, d1, d2 = (i + 1) % 3, (i + 2) % 3, (d + 1) % 3, (d + 2) % 3
+        return jac[i1][d1] * jac[i2][d2] - jac[i1][d2] * jac[i2][d1]
+
+    def normal(entries, speed):
+        return entries[0] * speed[0] + entries[1] * speed[1] + entries[2] * speed[2]
+
+    def face_flux(p, d):
+        jac = jacobian(p, [k for k in range(3) if k != d])
         speed = [rows(15 + i, p) for i in range(3)]
-        entries = [[metric(d, i) for i in range(3)] for d in range(3)]
-        det = (
+        fl_ref[d - 1, p, 0:5, :] = normal([metric(jac, d, i) for i in range(3)], speed)
+
+    def metrics(p):
+        jac = jacobian(p, range(3))
+        speed = [rows(15 + i, p) for i in range(3)]
+        entries = [[metric(jac, d, i) for i in range(3)] for d in range(3)]
+        det_ref[:, p, :] = (
             jac[0][0] * entries[0][0] + jac[0][1] * entries[1][0] + jac[0][2] * entries[2][0]
         )
-        det_ref[:, p, :] = det
         for d in range(3):
-            value = (
-                entries[d][0] * speed[0] + entries[d][1] * speed[1] + entries[d][2] * speed[2]
-            )
-            flux_ref[:, d, p, :] = value
-            if d > 0:
-                fl_ref[d - 1, p, 0:5, :] = value
+            flux_ref[:, d, p, :] = normal(entries[d], speed)
 
     fl_ref[...] = jnp.zeros_like(fl_ref)
     for p in range(64):
-        metrics(p)
+        if p % 4 in (0, 3):
+            face_flux(p, 2)
+        if (p // 4) % 4 in (0, 3):
+            face_flux(p, 1)
 
     lane = lax.broadcasted_iota(jnp.int32, (8, 128), 1)
 
@@ -525,6 +605,14 @@
     ]
     for copy in copies6:
         copy.start()
+    for p in range(64):
+        metrics(p)
+    stores = [
+        pltpu.make_async_copy(det_ref, det_out, store.at[0]),
+        pltpu.make_async_copy(flux_ref, flux_out, store.at[1]),
+    ]
+    for copy in stores:
+        copy.start()
     for copy in copies6:
         copy.wait_recv()
     for copy in copies6:
@@ -546,12 +634,15 @@
             value = 0.5 * (own - other)
             for q in range(4):
                 face_ref[t, :, a * 4 + q, :] = value[0:5, q * 32 : (q + 1) * 32]
+    for copy in stores:
+        copy.wait()
 
 
 def on_device(
     node_pos, ctrl_pos, ctrl_ids, wing_shift, wing_speed, minv, conn, face_elem, face_match
 ):
     vmem = pl.BlockSpec(memory_space=pltpu.VMEM)
+    hbm = pl.BlockSpec(memory_space=pltpu.HBM)
     dma = pltpu.SemaphoreType.DMA
     det, flux, face = pl.pallas_call(
         kernel,
@@ -560,9 +651,21 @@
             jax.ShapeDtypeStruct((5, 3, 64, 128), F32),
             jax.ShapeDtypeStruct((4, 5, 16, 32), F32),
         ),
-        in_specs=[vmem] * 9,
-        out_specs=[vmem] * 3,
+        in_specs=[hbm] * 10,
+        out_specs=[hbm, hbm, vmem],
         scratch_shapes=[
+            pltpu.VMEM((1, 32), jnp.int32),
+            pltpu.VMEM((3, 32), F32),
+            pltpu.VMEM((3, 2048), F32),
+            pltpu.VMEM((15, 1024), F32),
+            pltpu.VMEM((15, 1024), F32),
+            pltpu.VMEM((32, 8192), F32),
+            pltpu.VMEM((64, 128), jnp.int32),
+            pltpu.VMEM((4, 32), jnp.int32),
+            pltpu.VMEM((4, 32), jnp.int32),
+            pltpu.VMEM((4, 512, 256), BF16),
+            pltpu.VMEM((5, 64, 128), F32),
+            pltpu.VMEM((5, 3, 64, 128), F32),
             pltpu.VMEM((1, 1, 128), F32),
             pltpu.VMEM((DEVICES, 1, 128), F32),
             pltpu.VMEM((DEVICES, 8, 128), F32),
@@ -577,9 +680,9 @@
             pltpu.VMEM((32, 64, DEVICES), BF16),
             pltpu.VMEM((STORED, TILES, 256, 256), BF16),
             pltpu.VMEM((STORED, TILES, 256, 256), BF16),
-            pltpu.VMEM((3, DEVICES, 128), F32),
-            pltpu.VMEM((3, DEVICES, 128), F32),
-            pltpu.VMEM((3, 2048), F32),
+            pltpu.VMEM((2, DEVICES, 256), BF16),
+            pltpu.VMEM((4, DEVICES, 256), BF16),
+            pltpu.VMEM((32, 2048), BF16),
             pltpu.VMEM((96, 2048), BF16),
             pltpu.VMEM((64 * 32, 128), F32),
             pltpu.VMEM((2, 64, 8, 128), F32),
@@ -597,6 +700,8 @@
             dma((16,)),
             dma((4,)),
             dma((4,)),
+            dma((10,)),
+            dma((2,)),
         ],
         compiler_params=pltpu.CompilerParams(
             collective_id=0, has_side_effects=True, vmem_limit_bytes=66 * 1000 * 1000
@@ -612,6 +717,7 @@
         conn,
         face_elem.reshape(4, 32),
         face_match.reshape(4, 32),
+        selection(),
     )
     return det, flux, face.reshape(1, 1, 4, 5, 16, 32)
 

time: 80.6 us -> 70.9 us (0.88)
  Pallas kernels: 75.6 us -> 66 us
    pallas_call x1, Pallas kernels: 75.6 us -> 66 us  [on_device(): pl.pallas_call(kernel, out_shape=(jax.ShapeDtypeStruct((5, 64, 128), F32)...]
where the time goes in v2:
time: 70.9 us; the launch traced here: 70.8 us
  Pallas kernels  66 us (93%)
  local copies, waits for them, and re-layouts  4.15 us (6%)
    pallas_call x1, Pallas kernels, on_device(): pl.pallas_call(kernel, out_shape=(jax.ShapeDtypeStruct((5, 64, 128), F32)...  66 us
    unnamed x5, local copies, waits for them, and re-layouts  4.15 us

profile of v2, /device:TPU:1, one launch (start us, length us, event | category | flops | bytes accessed | tf_op | source)
XLA Modules:
  0.0 70.8 jit_solution(11696102877505338217)
XLA Ops:
  0.6 66.0 %wing.1 = (f32[5,64,128]{2,1,0:T(8,128)}, f32[5,3,64,128]{3,2,1,0:T(8,128)}, f32[4,5,16,32]{3,2,1,0:T(8,128)}) custom-call(s32[1,32]{1,0:T(1,128)} %bitcast.7, f32[3,32]{1,0:T(4,128)} %ctrl_in.1, f32[3,2048]{1,0:T(4,128)} %nodes_in.1, f32[15,1024]{1,0:T(8,128)} %shift_in.1, f32[15,1024]{1,0:T(8,128)} %speed_in.1, f32[32,8192]{1,0:T(8,128)} %minv_in.1, ...), custom_call_target="tpu_custom_call" | custom-call | tf_op jit(solution)/shard_map/wing/pallas_call | solution.py:647
  66.6 1.6 %copy.16 = f32[5,64,128]{2,1,0:T(8,128)} copy(f32[5,64,128]{2,1,0:T(8,128)} %get-tuple-element.12) | data formatting | bytes 327680
  68.2 0.0 copy-start
  68.2 1.9 %copy.17 = f32[5,3,64,128]{3,2,1,0:T(8,128)} copy(f32[5,3,64,128]{3,2,1,0:T(8,128)} %get-tuple-element.13) | data formatting | bytes 983040
  70.1 0.0 copy-done
  70.1 0.7 copy.18
Async XLA Ops:
  68.2 1.9 %copy-start = (f32[4,5,16,32]{3,2,1,0:T(8,128)S(1)}, f32[4,5,16,32]{3,2,1,0:T(8,128)}, u32[]{:S(2)}) copy-start(f32[4,5,16,32]{3,2,1,0:T(8,128)} %get-tuple-element.8) | copy-start | bytes 122884

commit v3 on v2

--- a/solution.py
+++ b/solution.py
@@ -24,13 +24,15 @@
 CROSS = float(2.0 * HALF_INV * np.log2(np.e))
 STORED = 24
 TILES = 8
+R_PERMUTED = 24
+R_UNITS = (64 - R_PERMUTED) // 4
 
 
 PAIRS = ((0, 0), (0, 1), (0, 2), (1, 0), (1, 1), (2, 0))
 
 
 def selection():
-    chosen = np.zeros((4, 512, 256), np.float32)
+    chosen = np.zeros((4, 384, 256), np.float32)
     for g in range(4):
         for l in range(8):
             for j, (part, _) in enumerate(PAIRS):
@@ -111,6 +113,7 @@
     gp_ref,
     idr_ref,
     table_ref,
+    plain_ref,
     r3_ref,
     m3_ref,
     cross_ref,
@@ -123,22 +126,13 @@
     lhs_ref,
     nb_ref,
     t3_ref,
+    tab_ref,
     gat_ref,
     fl_ref,
     tr_ref,
     rc_ref,
-    send1,
-    recv1,
-    send2,
-    recv2,
-    send3,
+    sems,
     recv3,
-    send4,
-    recv4,
-    send5,
-    recv5,
-    send6,
-    recv6,
     load,
     store,
 ):
@@ -201,6 +195,7 @@
     table = jnp.concatenate(
         [shift_ref[...], speed_ref[...], jnp.zeros((2, shift_ref.shape[1]), F32)], axis=0
     )
+    plain_ref[...] = table
     for k, part in enumerate(split3(table)):
         table_ref[k * 32 : (k + 1) * 32, :] = part
 
@@ -210,8 +205,8 @@
         return pltpu.make_async_remote_copy(
             src_ref=own_ref,
             dst_ref=g1_ref.at[pl.ds(group * GROUP + place, 1)],
-            send_sem=send1.at[k],
-            recv_sem=recv1.at[k],
+            send_sem=sems.at[0],
+            recv_sem=sems.at[1],
             device_id=device,
             device_id_type=MESH,
         )
@@ -227,16 +222,27 @@
     nb_ref[...] = jnp.concatenate(
         [node_parts[part].astype(F32) for _, part in PAIRS] + [jnp.zeros((14, 2048), F32)], axis=0
     ).astype(BF16)
-    for copy in copies1:
-        copy.wait_recv()
+    def all_rows(ref, count, sent, received):
+        return pltpu.make_async_remote_copy(
+            src_ref=ref.at[pl.ds(0, count)],
+            dst_ref=ref.at[pl.ds(0, count)],
+            send_sem=sems.at[sent],
+            recv_sem=sems.at[received],
+            device_id=partner,
+            device_id_type=MESH,
+        )
+
+    every1 = all_rows(g1_ref, len(line), 0, 1)
+    every2 = all_rows(g1_ref, len(plane) * GROUP, 2, 3)
+    every1.wait_recv()
 
     def second_copy(k, device):
         rows = pl.ds(group * GROUP, GROUP)
         return pltpu.make_async_remote_copy(
             src_ref=g1_ref.at[rows],
             dst_ref=g1_ref.at[rows],
-            send_sem=send2.at[k],
-            recv_sem=recv2.at[k],
+            send_sem=sems.at[2],
+            recv_sem=sems.at[3],
             device_id=device,
             device_id_type=MESH,
         )
@@ -244,12 +250,9 @@
     copies2 = [second_copy(k, plane_device(*d)) for k, d in enumerate(plane)]
     for copy in copies2:
         copy.start()
-    for copy in copies1:
-        copy.wait_send()
-    for copy in copies2:
-        copy.wait_recv()
-    for copy in copies2:
-        copy.wait_send()
+    every1.wait_send()
+    every2.wait_recv()
+    every2.wait_send()
 
     gp_ref[...] = g1_ref[...].reshape(DEVICES, 128)
     for ny in range(NY):
@@ -257,6 +260,23 @@
             [gp_ref[(ny * NX + q) * GROUP : (ny * NX + q + 1) * GROUP, 0:32] for q in range(NX)],
             axis=1,
         )
+
+    def permuted(source_ref, index, blocks):
+        node = jnp.broadcast_to(index, (8, 128))
+        lane = node & 127
+        block = node >> 7
+        found = [None] * 4
+        for k in range(blocks):
+            here = block == k
+            for r in range(4):
+                taken = jnp.take_along_axis(
+                    source_ref[r * 8 : r * 8 + 8, k * 128 : (k + 1) * 128],
+                    lane,
+                    axis=1,
+                    mode="promise_in_bounds",
+                )
+                found[r] = taken if k == 0 else jnp.where(here, taken, found[r])
+        return found
 
     def selected(accs, parts_ref, index, blocks, which):
         spread = one_hot(index, blocks)
@@ -273,16 +293,22 @@
             pltpu.matmul_pop(acc)
 
         def right_side(i, carry):
-            for u in range(8):
-                pair = idr_ref[pl.ds((i * 8 + u) * 2, 2), :]
+            for u in range(R_UNITS):
+                pair = idr_ref[pl.ds((i * R_UNITS + u) * 2, 2), :]
                 index = jnp.concatenate([pair[0:1], pair[1:2]], axis=1)
                 selected(accs, table_ref, index, 8, u)
-            for u in range(8):
-                lanes = pl.ds(pl.multiple_of((i * 8 + u) * 256, 256), 256)
+            for v in range(R_PERMUTED // 2):
+                row = 64 - R_PERMUTED + i * (R_PERMUTED // 2) + v
+                lanes = pl.ds(pl.multiple_of(row * 128, 128), 128)
+                found = permuted(plain_ref, idr_ref[pl.ds(row, 1), :].astype(jnp.int32), 8)
+                for k, part in enumerate(split3(jnp.concatenate(found, axis=0))):
+                    r3_ref[k * 32 : (k + 1) * 32, lanes] = part
+            for u in range(R_UNITS):
+                lanes = pl.ds(pl.multiple_of((i * R_UNITS + u) * 256, 256), 256)
                 r3_ref[:, lanes] = pltpu.matmul_pop(accs[u]).astype(BF16)
             return carry
 
-        lax.fori_loop(0, 4, right_side, 0)
+        lax.fori_loop(0, 2, right_side, 0)
 
         for k in range(32):
             lanes = slice(k * 256, (k + 1) * 256)
@@ -295,7 +321,7 @@
             pltpu.matmul_acc_lhs(accs[k % 2], m3_ref[:, lanes], load_staged_rhs=0)
         cross_ref[...] = pltpu.matmul_pop(accs[0]) + pltpu.matmul_pop(accs[1])
 
-    pl.run_scoped(first_stage, *[pltpu.ACC(u % 2)((96, 256), F32) for u in range(8)])
+    pl.run_scoped(first_stage, *[pltpu.ACC(u % 2)((96, 256), F32) for u in range(R_UNITS)])
     cross = cross_ref[...]
 
     def piece(a, b):
@@ -314,7 +340,7 @@
         return pltpu.make_async_remote_copy(
             src_ref=g2_ref.at[pl.ds(mine, 1)],
             dst_ref=g2_ref.at[pl.ds(mine, 1)],
-            send_sem=send3.at[k],
+            send_sem=sems.at[4],
             recv_sem=recv3.at[k],
             device_id=device,
             device_id_type=MESH,
@@ -324,8 +350,27 @@
     for copy in copies3:
         copy.start()
 
-    def weights_of(power):
-        value = jnp.exp2(power)
+    def block_rows(of_y, of_x, of_core):
+        return pl.ds((of_y * NX + of_x) * GROUP + of_core * NZ, NZ)
+
+    def fourth_copy(k, device, rows):
+        return pltpu.make_async_remote_copy(
+            src_ref=g2_ref.at[rows],
+            dst_ref=g2_ref.at[rows],
+            send_sem=sems.at[5],
+            recv_sem=sems.at[6],
+            device_id=device,
+            device_id_type=MESH,
+        )
+
+    def forward(step):
+        row = group * GROUP + core * NZ + lax.rem(z + NZ - step, NZ)
+        for k, d in enumerate(plane):
+            fourth_copy(k, plane_device(*d), pl.ds(row, 1)).start()
+
+    forward(0)
+
+    def parts_of(value):
         high = value.astype(BF16)
         return high, (value - high.astype(F32)).astype(BF16)
 
@@ -341,13 +386,14 @@
         def step(t, carry):
             lanes = pl.ds(pl.multiple_of(t * 256, 256), 256)
             for l in range(8):
+                used = [accs[l % 2][(l // 2 * 3 + g) % 4] for g in range(3)]
                 pltpu.matmul_push_rhs(cross_rhs(l, lanes), staging_register=0, mxu_index=l % 2)
                 for g in range(3):
                     pltpu.matmul_acc_lhs(
-                        accs[l % 2][g], lhs_ref[g], load_staged_rhs=0 if g == 0 else None
+                        used[g], lhs_ref[g], load_staged_rhs=0 if g == 0 else None
                     )
                 for g in range(3):
-                    high, low = weights_of(pltpu.matmul_pop(accs[l % 2][g]))
+                    high, low = parts_of(jnp.exp2(pltpu.matmul_pop(used[g])))
                     kh_ref[g * 8 + l, t] = high
                     kl_ref[g * 8 + l, t] = low
             return carry
@@ -359,9 +405,10 @@
             pltpu.matmul_pop(acc)
         for g in range(4):
             for k in range(2):
-                pltpu.matmul_push_rhs(
-                    sel_ref[g, k * 256 : (k + 1) * 256, :], staging_register=0, mxu_index=g % 2
-                )
+                chosen = sel_ref[g, k * 256 : min((k + 1) * 256, 384), :]
+                if k == 1:
+                    chosen = jnp.concatenate([chosen, jnp.zeros((128, 256), BF16)], axis=0)
+                pltpu.matmul_push_rhs(chosen, staging_register=0, mxu_index=g % 2)
                 pltpu.matmul_acc_lhs(accs[g], parts_ref[k], load_staged_rhs=0)
         for g in range(4):
             lhs_ref[g] = pltpu.matmul_pop(accs[g]).astype(BF16)
@@ -374,8 +421,8 @@
 
         pl.run_scoped(
             scoped,
-            tuple(pltpu.ACC(0)((256, 256), F32) for _ in range(3)),
-            tuple(pltpu.ACC(1)((256, 256), F32) for _ in range(3)),
+            tuple(pltpu.ACC(0)((256, 256), F32) for _ in range(4)),
+            tuple(pltpu.ACC(1)((256, 256), F32) for _ in range(4)),
         )
 
     for k, part in enumerate(split3(gp_ref[...])):
@@ -383,57 +430,45 @@
     parts_ref[1, :, 128:256] = jnp.zeros((DEVICES, 128), BF16)
     pl.run_scoped(start_generation, *[pltpu.ACC(g % 2)((256, 256), F32) for g in range(4)])
 
-    generate_range(0, 3)
-    for copy in copies3:
-        copy.wait_recv()
-
-    def block_rows(of_y, of_x, of_core):
-        return pl.ds((of_y * NX + of_x) * GROUP + of_core * NZ, NZ)
-
-    def fourth_copy(k, device):
-        rows = block_rows(y, x, core)
-        return pltpu.make_async_remote_copy(
-            src_ref=g2_ref.at[rows],
-            dst_ref=g2_ref.at[rows],
-            send_sem=send4.at[k],
-            recv_sem=recv4.at[k],
-            device_id=device,
-            device_id_type=MESH,
-        )
-
-    copies4 = [fourth_copy(k, plane_device(*d)) for k, d in enumerate(plane)]
-    for copy in copies4:
-        copy.start()
+    generate_range(0, 2)
+
+    for step in (1, 7, 2, 6):
+        copies3[step - 1].wait_recv()
+        forward(step)
+    generate_range(2, 3)
+    for step in (3, 5, 4):
+        copies3[step - 1].wait_recv()
+        forward(step)
+    every3 = all_rows(g2_ref, NZ - 1, 4, 4)
+    every4 = all_rows(g2_ref, NZ * len(plane), 5, 6)
+    every5 = all_rows(g2_ref, NZ * NX * NY, 7, 8)
 
     def fifth_copy(k, dy, dx):
         rows = block_rows(lax.rem(y + NY - dy, NY), lax.rem(x + NX - dx, NX), core)
         return pltpu.make_async_remote_copy(
             src_ref=g2_ref.at[rows],
             dst_ref=g2_ref.at[rows],
-            send_sem=send5.at[k],
-            recv_sem=recv5.at[k],
+            send_sem=sems.at[7],
+            recv_sem=sems.at[8],
             device_id=partner,
             device_id_type=MESH,
         )
 
     copies5 = [fifth_copy(k, *d) for k, d in enumerate([(0, 0)] + plane)]
     copies5[0].start()
-    for copy in copies3:
-        copy.wait_send()
-    generate_range(3, 8)
-    for k in range(len(plane)):
-        copies4[k].wait_recv()
-        copies5[k + 1].start()
-    for copy in copies4:
-        copy.wait_send()
+    every3.wait_send()
+    generate_range(3, 7)
+    every4.wait_recv()
+    for copy in copies5[1:]:
+        copy.start()
+    every4.wait_send()
+    generate_range(7, 8)
     turned = gp_ref[...].T
     scale_ref[...] = jnp.exp(
         -HALF_INV * (turned[32:64] ** 2 + turned[64:96] ** 2 + turned[96:128] ** 2)
     )
-    for copy in copies5:
-        copy.wait_recv()
-    for copy in copies5:
-        copy.wait_send()
+    every5.wait_recv()
+    every5.wait_send()
 
     for j in range(8):
         block = g2_ref[:, j, :].T
@@ -444,72 +479,89 @@
             wc_ref[l, 0:32, :] = high
             wc_ref[l, 32:64, :] = (value - high.astype(F32)).astype(BF16)
 
-    def products(zero, one, high_acc, low_acc):
+    def products(zero, one, high_accs, low_accs):
         accs = (zero, one)
-        for acc in (*zero, *one, high_acc, low_acc):
+        for acc in (*zero, *one, *high_accs, *low_accs):
             pltpu.matmul_pop(acc)
 
-        def add(l, high, low):
+        def add(u, l, high, low):
             pltpu.matmul_push_rhs(high, staging_register=0, mxu_index=0)
-            pltpu.matmul_acc_lhs(high_acc, wc_ref[l], load_staged_rhs=0)
+            pltpu.matmul_acc_lhs(high_accs[u], wc_ref[l], load_staged_rhs=0)
             pltpu.matmul_push_rhs(low, staging_register=0, mxu_index=1)
-            pltpu.matmul_acc_lhs(low_acc, wc_ref[l, 0:32], load_staged_rhs=0)
-
-        def columns(t, carry):
-            lanes = pl.ds(pl.multiple_of(t * 256, 256), 256)
-
-            def power(l):
-                pltpu.matmul_push_rhs(cross_rhs(l, lanes), staging_register=1, mxu_index=l % 2)
-                pltpu.matmul_acc_lhs(accs[l % 2][(l // 2) % 2], lhs_ref[3], load_staged_rhs=1)
+            pltpu.matmul_acc_lhs(low_accs[u], wc_ref[l, 0:32], load_staged_rhs=0)
+
+        def columns(i, carry):
+            lanes = [pl.ds(pl.multiple_of((2 * i + u) * 256, 256), 256) for u in range(2)]
+
+            def power(n):
+                u, l = n // 8, n % 8
+                pltpu.matmul_push_rhs(
+                    cross_rhs(l, lanes[u]), staging_register=1, mxu_index=n % 2
+                )
+                pltpu.matmul_acc_lhs(accs[n % 2][(n // 2) % 2], lhs_ref[3], load_staged_rhs=1)
 
             power(0)
             power(1)
-            for l in range(8):
-                high, low = weights_of(pltpu.matmul_pop(accs[l % 2][(l // 2) % 2]))
-                if l < 6:
-                    power(l + 2)
+            for n in range(16):
+                u, l = n // 8, n % 8
+                t = 2 * i + u
+                value = jnp.exp2(pltpu.matmul_pop(accs[n % 2][(n // 2) % 2]))
+                if n < 14:
+                    power(n + 2)
                 for k in range(3 * l, 3 * l + 3):
-                    add(k, kh_ref[k, t], kl_ref[k, t])
-                add(24 + l, high, low)
-            first = pltpu.matmul_pop(high_acc)
-            total = first[0:32] + first[32:64] + pltpu.matmul_pop(low_acc)
-            place_of = nodes_ref[:, lanes]
-            factor = jnp.exp(-HALF_INV * jnp.sum(place_of * place_of, axis=0, keepdims=True))
-            base = jnp.concatenate([place_of] * 5 + [jnp.zeros((17, 256), F32)], axis=0)
-            for k, part in enumerate(split3(total * factor + base)):
-                t3_ref[k * 32 : (k + 1) * 32, lanes] = part
+                    add(u, k, kh_ref[k, t], kl_ref[k, t])
+                add(u, 24 + l, *parts_of(value))
+            for u in range(2):
+                first = pltpu.matmul_pop(high_accs[u])
+                total = first[0:32] + first[32:64] + pltpu.matmul_pop(low_accs[u])
+                place_of = nodes_ref[:, lanes[u]]
+                factor = jnp.exp(
+                    -HALF_INV * jnp.sum(place_of * place_of, axis=0, keepdims=True)
+                )
+                base = jnp.concatenate([place_of] * 5 + [jnp.zeros((17, 256), F32)], axis=0)
+                moved = total * factor + base
+                tab_ref[:, lanes[u]] = moved
+                for k, part in enumerate(split3(moved)):
+                    t3_ref[k * 32 : (k + 1) * 32, lanes[u]] = part
             return carry
 
-        lax.fori_loop(0, TILES, columns, 0)
+        lax.fori_loop(0, TILES // 2, columns, 0)
 
     pl.run_scoped(
         products,
         tuple(pltpu.ACC(0)((256, 256), F32) for _ in range(2)),
         tuple(pltpu.ACC(1)((256, 256), F32) for _ in range(2)),
-        pltpu.ACC(0)((64, 256), F32),
-        pltpu.ACC(1)((32, 256), F32),
-    )
-
-    def last_stage(*accs):
-        for acc in accs:
-            pltpu.matmul_pop(acc)
-
-        def gather(i, carry):
-            for u in range(8):
-                pair = conn_ref[pl.ds((i * 8 + u) * 2, 2), :].astype(F32)
-                index = jnp.concatenate([pair[0:1], pair[1:2]], axis=1)
-                selected(accs, t3_ref, index, 16, u)
-            for u in range(8):
-                parts = pltpu.matmul_pop(accs[u])
-                value = parts[0:32] + parts[32:64] + parts[64:96]
-                first = (i * 8 + u) * 64
-                gat_ref[pl.ds(first, 32), :] = value[:, 0:128]
-                gat_ref[pl.ds(first + 32, 32), :] = value[:, 128:256]
-            return carry
-
-        lax.fori_loop(0, 4, gather, 0)
-
-    pl.run_scoped(last_stage, *[pltpu.ACC(u % 2)((96, 256), F32) for u in range(8)])
+        tuple(pltpu.ACC(0)((64, 256), F32) for _ in range(2)),
+        tuple(pltpu.ACC(1)((32, 256), F32) for _ in range(2)),
+    )
+
+    def gather(accs, by_matmul, by_permute):
+        for u, (p, q) in enumerate(by_matmul):
+            index = jnp.concatenate([conn_ref[p : p + 1, :], conn_ref[q : q + 1, :]], axis=1)
+            selected(accs, t3_ref, index.astype(F32), 16, u)
+        for p in by_permute:
+            for r, value in enumerate(permuted(tab_ref, conn_ref[p : p + 1, :], 16)):
+                gat_ref[p * 32 + r * 8 : p * 32 + r * 8 + 8, :] = value
+        for u, (p, q) in enumerate(by_matmul):
+            parts = pltpu.matmul_pop(accs[u])
+            value = parts[0:32] + parts[32:64] + parts[64:96]
+            gat_ref[p * 32 : p * 32 + 32, :] = value[:, 0:128]
+            gat_ref[q * 32 : q * 32 + 32, :] = value[:, 128:256]
+
+    inside = [p for p in range(64) if p % 4 in (1, 2) and (p // 4) % 4 in (1, 2)]
+    outside = [p for p in range(64) if p not in inside]
+
+    def gather_stage(points, count):
+        pairs = [(points[2 * u], points[2 * u + 1]) for u in range(count)]
+
+        def scoped(*accs):
+            for acc in accs:
+                pltpu.matmul_pop(acc)
+            gather(accs, pairs, points[2 * count :])
+
+        pl.run_scoped(scoped, *[pltpu.ACC(u % 2)((96, 256), F32) for u in range(count)])
+
+    gather_stage(outside, 16)
 
     derivative = lobatto_derivative()
 
@@ -596,8 +648,8 @@
         pltpu.make_async_remote_copy(
             src_ref=tr_ref.at[t],
             dst_ref=rc_ref.at[slot],
-            send_sem=send6.at[t],
-            recv_sem=recv6.at[slot],
+            send_sem=sems.at[9],
+            recv_sem=sems.at[10],
             device_id=device,
             device_id_type=MESH,
         )
@@ -605,6 +657,7 @@
     ]
     for copy in copies6:
         copy.start()
+    gather_stage(inside, 4)
     for p in range(64):
         metrics(p)
     stores = [
@@ -613,10 +666,16 @@
     ]
     for copy in stores:
         copy.start()
-    for copy in copies6:
-        copy.wait_recv()
-    for copy in copies6:
-        copy.wait_send()
+    every6 = pltpu.make_async_remote_copy(
+        src_ref=tr_ref,
+        dst_ref=rc_ref,
+        send_sem=sems.at[9],
+        recv_sem=sems.at[10],
+        device_id=partner,
+        device_id_type=MESH,
+    )
+    every6.wait_recv()
+    every6.wait_send()
 
     for t in range(4):
         index = jnp.broadcast_to(
@@ -631,9 +690,42 @@
                 other = jnp.where(
                     jnp.broadcast_to(span == NY * NCORE - 1, (8, 128)), -own, other
                 )
-            value = 0.5 * (own - other)
+            face_ref[t, a] = 0.5 * (own - other)
+    for copy in stores:
+        copy.wait()
+
+
+def finish(
+    det_in,
+    flux_in,
+    packed_in,
+    det_out,
+    flux_out,
+    face_out,
+    det_ref,
+    flux_ref,
+    packed_ref,
+    face_ref,
+    sem,
+):
+    pairs = ((det_in, det_ref, det_out), (flux_in, flux_ref, flux_out))
+    packed = pltpu.make_async_copy(packed_in, packed_ref, sem.at[5])
+    packed.start()
+    loads = [pltpu.make_async_copy(a, b, sem.at[k]) for k, (a, b, _) in enumerate(pairs)]
+    stores = [pltpu.make_async_copy(b, c, sem.at[k + 2]) for k, (_, b, c) in enumerate(pairs)]
+    for copy in loads:
+        copy.start()
+    packed.wait()
+    for t in range(4):
+        for a in range(4):
+            value = packed_ref[t, a]
             for q in range(4):
                 face_ref[t, :, a * 4 + q, :] = value[0:5, q * 32 : (q + 1) * 32]
+    for k in range(2):
+        loads[k].wait()
+        stores[k].start()
+    stores.append(pltpu.make_async_copy(face_ref, face_out, sem.at[4]))
+    stores[2].start()
     for copy in stores:
         copy.wait()
 
@@ -644,12 +736,12 @@
     vmem = pl.BlockSpec(memory_space=pltpu.VMEM)
     hbm = pl.BlockSpec(memory_space=pltpu.HBM)
     dma = pltpu.SemaphoreType.DMA
-    det, flux, face = pl.pallas_call(
+    det, flux, packed = pl.pallas_call(
         kernel,
         out_shape=(
             jax.ShapeDtypeStruct((5, 64, 128), F32),
             jax.ShapeDtypeStruct((5, 3, 64, 128), F32),
-            jax.ShapeDtypeStruct((4, 5, 16, 32), F32),
+            jax.ShapeDtypeStruct((4, 4, 8, 128), F32),
         ),
         in_specs=[hbm] * 10,
         out_specs=[hbm, hbm, vmem],
@@ -663,7 +755,7 @@
             pltpu.VMEM((64, 128), jnp.int32),
             pltpu.VMEM((4, 32), jnp.int32),
             pltpu.VMEM((4, 32), jnp.int32),
-            pltpu.VMEM((4, 512, 256), BF16),
+            pltpu.VMEM((4, 384, 256), BF16),
             pltpu.VMEM((5, 64, 128), F32),
             pltpu.VMEM((5, 3, 64, 128), F32),
             pltpu.VMEM((1, 1, 128), F32),
@@ -672,6 +764,7 @@
             pltpu.VMEM((DEVICES, 128), F32),
             pltpu.VMEM((64, 128), F32),
             pltpu.VMEM((96, 1024), BF16),
+            pltpu.VMEM((32, 1024), F32),
             pltpu.VMEM((96, 8192), BF16),
             pltpu.VMEM((96, 8192), BF16),
             pltpu.VMEM((96, 256), F32),
@@ -684,27 +777,18 @@
             pltpu.VMEM((4, DEVICES, 256), BF16),
             pltpu.VMEM((32, 2048), BF16),
             pltpu.VMEM((96, 2048), BF16),
+            pltpu.VMEM((32, 2048), F32),
             pltpu.VMEM((64 * 32, 128), F32),
             pltpu.VMEM((2, 64, 8, 128), F32),
             pltpu.VMEM((4, 4, 8, 128), F32),
             pltpu.VMEM((4, 4, 8, 128), F32),
-            dma((15,)),
-            dma((15,)),
-            dma((15,)),
-            dma((15,)),
+            dma((11,)),
             dma((7,)),
-            dma((7,)),
-            dma((15,)),
-            dma((15,)),
-            dma((16,)),
-            dma((16,)),
-            dma((4,)),
-            dma((4,)),
             dma((10,)),
             dma((2,)),
         ],
         compiler_params=pltpu.CompilerParams(
-            collective_id=0, has_side_effects=True, vmem_limit_bytes=66 * 1000 * 1000
+            collective_id=0, has_side_effects=True, vmem_limit_bytes=67043328
         ),
         name="wing",
     )(
@@ -719,6 +803,24 @@
         face_match.reshape(4, 32),
         selection(),
     )
+    det, flux, face = pl.pallas_call(
+        finish,
+        out_shape=(
+            jax.ShapeDtypeStruct((5, 64, 128), F32),
+            jax.ShapeDtypeStruct((5, 3, 64, 128), F32),
+            jax.ShapeDtypeStruct((4, 5, 16, 32), F32),
+        ),
+        in_specs=[hbm] * 3,
+        out_specs=[hbm] * 3,
+        scratch_shapes=[
+            pltpu.VMEM((5, 64, 128), F32),
+            pltpu.VMEM((5, 3, 64, 128), F32),
+            pltpu.VMEM((4, 4, 8, 128), F32),
+            pltpu.VMEM((4, 5, 16, 32), F32),
+            dma((6,)),
+        ],
+        name="wing_end",
+    )(det, flux, packed)
     return det, flux, face.reshape(1, 1, 4, 5, 16, 32)
 
 

time: 70.9 us -> 61.6 us (0.87)
  Pallas kernels: 66 us -> 60.6 us
  local copies, waits for them, and re-layouts: 4.15 us -> 0 us
    pallas_call x1, Pallas kernels: 66 us -> 58.5 us  [on_device(): pl.pallas_call(kernel, out_shape=(jax.ShapeDtypeStruct((5, 64, 128), F32)...]
    unnamed x5 -> x0, local copies, waits for them, and re-layouts: 4.15 us -> none
    pallas_call x0 -> x1, Pallas kernels: none -> 2.1 us  [on_device(): pl.pallas_call(finish, out_shape=(jax.ShapeDtypeStruct((5, 64, 128), F32)...]
where the time goes in v3:
time: 61.6 us; the launch traced here: 61.4 us
  Pallas kernels  60.6 us (98%)
  between operations  0.8 us (1%)
    pallas_call x1, Pallas kernels, on_device(): pl.pallas_call(kernel, out_shape=(jax.ShapeDtypeStruct((5, 64, 128), F32)...  58.5 us
    pallas_call x1, Pallas kernels, on_device(): pl.pallas_call(finish, out_shape=(jax.ShapeDtypeStruct((5, 64, 128), F32)...  2.1 us

profile of v3, /device:TPU:1, one launch (start us, length us, event | category | flops | bytes accessed | tf_op | source)
XLA Modules:
  0.0 61.4 jit_solution(5861884756540433391)
XLA Ops:
  0.6 58.5 %wing.1 = (f32[5,64,128]{2,1,0:T(8,128)}, f32[5,3,64,128]{3,2,1,0:T(8,128)}, f32[4,4,8,128]{3,2,1,0:T(8,128)}) custom-call(s32[1,32]{1,0:T(1,128)} %bitcast.6, f32[3,32]{1,0:T(4,128)} %ctrl_in.1, f32[3,2048]{1,0:T(4,128)} %nodes_in.1, f32[15,1024]{1,0:T(8,128)} %shift_in.1, f32[15,1024]{1,0:T(8,128)} %speed_in.1, f32[32,8192]{1,0:T(8,128)} %minv_in.1, ...), custom_call_target="tpu_custom_call" | custom-call | tf_op jit(solution)/shard_map/wing/pallas_call | solution.py:739
  59.2 2.1 %wing_end.1 = (f32[5,64,128]{2,1,0:T(8,128)}, f32[5,3,64,128]{3,2,1,0:T(8,128)}, f32[4,5,16,32]{3,2,1,0:T(8,128)}) custom-call(f32[5,64,128]{2,1,0:T(8,128)} %get-tuple-element.9.det_in, f32[5,3,64,128]{3,2,1,0:T(8,128)} %get-tuple-element.10.flux_in, f32[4,4,8,128]{3,2,1,0:T(8,128)} %get-tuple-element.11.packed_in), custom_call_target="tpu_custom_call" | custom-call | tf_op jit(solution)/shard_map/wing_end/pallas_call | solution.py:806

commit v4 on v3

--- a/solution.py
+++ b/solution.py
@@ -24,8 +24,9 @@
 CROSS = float(2.0 * HALF_INV * np.log2(np.e))
 STORED = 24
 TILES = 8
+COLUMNS = 2
 R_PERMUTED = 24
-R_UNITS = (64 - R_PERMUTED) // 4
+R_UNITS = (64 - R_PERMUTED) // 2
 
 
 PAIRS = ((0, 0), (0, 1), (0, 2), (1, 0), (1, 1), (2, 0))
@@ -292,13 +293,13 @@
         for acc in accs:
             pltpu.matmul_pop(acc)
 
-        def right_side(i, carry):
+        def right_side(i):
             for u in range(R_UNITS):
                 pair = idr_ref[pl.ds((i * R_UNITS + u) * 2, 2), :]
                 index = jnp.concatenate([pair[0:1], pair[1:2]], axis=1)
                 selected(accs, table_ref, index, 8, u)
-            for v in range(R_PERMUTED // 2):
-                row = 64 - R_PERMUTED + i * (R_PERMUTED // 2) + v
+            for v in range(R_PERMUTED):
+                row = 64 - R_PERMUTED + i * (R_PERMUTED) + v
                 lanes = pl.ds(pl.multiple_of(row * 128, 128), 128)
                 found = permuted(plain_ref, idr_ref[pl.ds(row, 1), :].astype(jnp.int32), 8)
                 for k, part in enumerate(split3(jnp.concatenate(found, axis=0))):
@@ -306,9 +307,8 @@
             for u in range(R_UNITS):
                 lanes = pl.ds(pl.multiple_of((i * R_UNITS + u) * 256, 256), 256)
                 r3_ref[:, lanes] = pltpu.matmul_pop(accs[u]).astype(BF16)
-            return carry
-
-        lax.fori_loop(0, 2, right_side, 0)
+
+        right_side(0)
 
         for k in range(32):
             lanes = slice(k * 256, (k + 1) * 256)
@@ -484,34 +484,43 @@
         for acc in (*zero, *one, *high_accs, *low_accs):
             pltpu.matmul_pop(acc)
 
+        turn = [0, 0]
+
+        def multiply(mxu, acc, lhs, rhs):
+            register = turn[mxu] % 2
+            turn[mxu] += 1
+            pltpu.matmul_push_rhs(rhs, staging_register=register, mxu_index=mxu)
+            pltpu.matmul_acc_lhs(acc, lhs, load_staged_rhs=register)
+
         def add(u, l, high, low):
-            pltpu.matmul_push_rhs(high, staging_register=0, mxu_index=0)
-            pltpu.matmul_acc_lhs(high_accs[u], wc_ref[l], load_staged_rhs=0)
-            pltpu.matmul_push_rhs(low, staging_register=0, mxu_index=1)
-            pltpu.matmul_acc_lhs(low_accs[u], wc_ref[l, 0:32], load_staged_rhs=0)
+            multiply(0, high_accs[u], wc_ref[l], high)
+            multiply(1, low_accs[u], wc_ref[l, 0:32], low)
 
         def columns(i, carry):
-            lanes = [pl.ds(pl.multiple_of((2 * i + u) * 256, 256), 256) for u in range(2)]
+            lanes = [
+                pl.ds(pl.multiple_of((COLUMNS * i + u) * 256, 256), 256) for u in range(COLUMNS)
+            ]
 
             def power(n):
                 u, l = n // 8, n % 8
-                pltpu.matmul_push_rhs(
-                    cross_rhs(l, lanes[u]), staging_register=1, mxu_index=n % 2
-                )
-                pltpu.matmul_acc_lhs(accs[n % 2][(n // 2) % 2], lhs_ref[3], load_staged_rhs=1)
+                multiply(n % 2, accs[n % 2][(n // 2) % 2], lhs_ref[3], cross_rhs(l, lanes[u]))
 
             power(0)
             power(1)
-            for n in range(16):
+            def stored(n):
                 u, l = n // 8, n % 8
-                t = 2 * i + u
-                value = jnp.exp2(pltpu.matmul_pop(accs[n % 2][(n // 2) % 2]))
-                if n < 14:
-                    power(n + 2)
+                t = COLUMNS * i + u
                 for k in range(3 * l, 3 * l + 3):
                     add(u, k, kh_ref[k, t], kl_ref[k, t])
+
+            for n in range(8 * COLUMNS):
+                u, l = n // 8, n % 8
+                value = jnp.exp2(pltpu.matmul_pop(accs[n % 2][(n // 2) % 2]))
+                if n < 8 * COLUMNS - 2:
+                    power(n + 2)
+                stored(n)
                 add(u, 24 + l, *parts_of(value))
-            for u in range(2):
+            for u in range(COLUMNS):
                 first = pltpu.matmul_pop(high_accs[u])
                 total = first[0:32] + first[32:64] + pltpu.matmul_pop(low_accs[u])
                 place_of = nodes_ref[:, lanes[u]]
@@ -525,14 +534,14 @@
                     t3_ref[k * 32 : (k + 1) * 32, lanes[u]] = part
             return carry
 
-        lax.fori_loop(0, TILES // 2, columns, 0)
+        lax.fori_loop(0, TILES // COLUMNS, columns, 0)
 
     pl.run_scoped(
         products,
         tuple(pltpu.ACC(0)((256, 256), F32) for _ in range(2)),
         tuple(pltpu.ACC(1)((256, 256), F32) for _ in range(2)),
-        tuple(pltpu.ACC(0)((64, 256), F32) for _ in range(2)),
-        tuple(pltpu.ACC(1)((32, 256), F32) for _ in range(2)),
+        tuple(pltpu.ACC(0)((64, 256), F32) for _ in range(COLUMNS)),
+        tuple(pltpu.ACC(1)((32, 256), F32) for _ in range(COLUMNS)),
     )
 
     def gather(accs, by_matmul, by_permute):
@@ -548,8 +557,9 @@
             gat_ref[p * 32 : p * 32 + 32, :] = value[:, 0:128]
             gat_ref[q * 32 : q * 32 + 32, :] = value[:, 128:256]
 
-    inside = [p for p in range(64) if p % 4 in (1, 2) and (p // 4) % 4 in (1, 2)]
-    outside = [p for p in range(64) if p not in inside]
+    chord_points = [p for p in range(64) if (p // 4) % 4 in (0, 3)]
+    span_points = [p for p in range(64) if p not in chord_points and p % 4 in (0, 3)]
+    inside = [p for p in range(64) if p not in chord_points + span_points]
 
     def gather_stage(points, count):
         pairs = [(points[2 * u], points[2 * u + 1]) for u in range(count)]
@@ -561,7 +571,7 @@
 
         pl.run_scoped(scoped, *[pltpu.ACC(u % 2)((96, 256), F32) for u in range(count)])
 
-    gather_stage(outside, 16)
+    gather_stage(chord_points, 10)
 
     derivative = lobatto_derivative()
 
@@ -609,13 +619,6 @@
         for d in range(3):
             flux_ref[:, d, p, :] = normal(entries[d], speed)
 
-    fl_ref[...] = jnp.zeros_like(fl_ref)
-    for p in range(64):
-        if p % 4 in (0, 3):
-            face_flux(p, 2)
-        if (p // 4) % 4 in (0, 3):
-            face_flux(p, 1)
-
     lane = lax.broadcasted_iota(jnp.int32, (8, 128), 1)
 
     def quarters(values):
@@ -624,7 +627,9 @@
             out = jnp.where(lane >= q * 32, values[q], out)
         return out
 
-    for t in range(4):
+    across = {0: (beside[1], 1), 1: (beside[0], 0), 2: (beside[3], 3), 3: (beside[2], 2)}
+
+    def trace(t):
         index = jnp.broadcast_to(
             jnp.concatenate([elem_ref[t : t + 1, :]] * 4, axis=1), (8, 128)
         )
@@ -643,8 +648,8 @@
             )
             tr_ref[t, a] = picked if t % 2 else -picked
 
-    across = [(0, beside[1], 1), (1, beside[0], 0), (2, beside[3], 3), (3, beside[2], 2)]
-    copies6 = [
+    def send(t):
+        device, slot = across[t]
         pltpu.make_async_remote_copy(
             src_ref=tr_ref.at[t],
             dst_ref=rc_ref.at[slot],
@@ -652,11 +657,23 @@
             recv_sem=sems.at[10],
             device_id=device,
             device_id_type=MESH,
-        )
-        for t, device, slot in across
-    ]
-    for copy in copies6:
-        copy.start()
+        ).start()
+
+    fl_ref[...] = jnp.zeros_like(fl_ref)
+    for p in chord_points:
+        face_flux(p, 1)
+    for t in (2, 3):
+        trace(t)
+    for t in (2, 3):
+        send(t)
+    gather_stage(span_points, 4)
+    for p in range(64):
+        if p % 4 in (0, 3):
+            face_flux(p, 2)
+    for t in (0, 1):
+        trace(t)
+    for t in (0, 1):
+        send(t)
     gather_stage(inside, 4)
     for p in range(64):
         metrics(p)

time: 61.6 us -> 60.2 us (0.977)
  Pallas kernels: 60.6 us -> 59.2 us
    pallas_call x1, Pallas kernels: 58.5 us -> 57.1 us  [on_device(): pl.pallas_call(kernel, out_shape=(jax.ShapeDtypeStruct((5, 64, 128), F32)...]
where the time goes in v4:
time: 60.2 us; the launch traced here: 60.1 us
  Pallas kernels  59.2 us (98%)
  between operations  0.82 us (1%)
    pallas_call x1, Pallas kernels, on_device(): pl.pallas_call(kernel, out_shape=(jax.ShapeDtypeStruct((5, 64, 128), F32)...  57.1 us
    pallas_call x1, Pallas kernels, on_device(): pl.pallas_call(finish, out_shape=(jax.ShapeDtypeStruct((5, 64, 128), F32)...  2.1 us

profile of v4, /device:TPU:1, one launch (start us, length us, event | category | flops | bytes accessed | tf_op | source)
XLA Modules:
  0.0 60.1 jit_solution(658300273013953229)
XLA Ops:
  0.6 57.1 %wing.1 = (f32[5,64,128]{2,1,0:T(8,128)}, f32[5,3,64,128]{3,2,1,0:T(8,128)}, f32[4,4,8,128]{3,2,1,0:T(8,128)}) custom-call(s32[1,32]{1,0:T(1,128)} %bitcast.6, f32[3,32]{1,0:T(4,128)} %ctrl_in.1, f32[3,2048]{1,0:T(4,128)} %nodes_in.1, f32[15,1024]{1,0:T(8,128)} %shift_in.1, f32[15,1024]{1,0:T(8,128)} %speed_in.1, f32[32,8192]{1,0:T(8,128)} %minv_in.1, ...), custom_call_target="tpu_custom_call" | custom-call | tf_op jit(solution)/shard_map/wing/pallas_call | solution.py:756
  57.8 2.1 %wing_end.1 = (f32[5,64,128]{2,1,0:T(8,128)}, f32[5,3,64,128]{3,2,1,0:T(8,128)}, f32[4,5,16,32]{3,2,1,0:T(8,128)}) custom-call(f32[5,64,128]{2,1,0:T(8,128)} %get-tuple-element.9.det_in, f32[5,3,64,128]{3,2,1,0:T(8,128)} %get-tuple-element.10.flux_in, f32[4,4,8,128]{3,2,1,0:T(8,128)} %get-tuple-element.11.packed_in), custom_call_target="tpu_custom_call" | custom-call | tf_op jit(solution)/shard_map/wing_end/pallas_call | solution.py:823

commit v5 on v4

--- a/solution.py
+++ b/solution.py
@@ -25,7 +25,7 @@
 STORED = 24
 TILES = 8
 COLUMNS = 2
-R_PERMUTED = 24
+R_PERMUTED = 32
 R_UNITS = (64 - R_PERMUTED) // 2
 
 
@@ -143,6 +143,8 @@
     line = [(dc, dz) for dc in range(NCORE) for dz in range(NZ) if (dc, dz) != (0, 0)]
     plane = [(dy, dx) for dy in range(NY) for dx in range(NX) if (dy, dx) != (0, 0)]
 
+    near = [dy != 2 and dx != 2 for dy, dx in plane]
+
     def line_device(dc, dz):
         return (y, lax.rem(core + dc, NCORE), lax.rem(z + dz, NZ), x)
 
@@ -187,19 +189,12 @@
     ]
     for copy in loads:
         copy.start()
-    for copy in loads[:4]:
+    for copy in loads[:2]:
         copy.wait()
     own_ref[0] = jnp.concatenate(
         [ids_ref[...].astype(F32)] + [ctrl_ref[k : k + 1, :] for k in range(3)], axis=1
     )
     g1_ref[group * GROUP + place] = own_ref[0]
-    table = jnp.concatenate(
-        [shift_ref[...], speed_ref[...], jnp.zeros((2, shift_ref.shape[1]), F32)], axis=0
-    )
-    plain_ref[...] = table
-    for k, part in enumerate(split3(table)):
-        table_ref[k * 32 : (k + 1) * 32, :] = part
-
     pl.semaphore_wait(barrier, len(greeted))
 
     def first_copy(k, device):
@@ -215,8 +210,14 @@
     copies1 = [first_copy(k, line_device(*d)) for k, d in enumerate(line)]
     for copy in copies1:
         copy.start()
-    for copy in loads[4:]:
+    for copy in loads[2:]:
         copy.wait()
+    table = jnp.concatenate(
+        [shift_ref[...], speed_ref[...], jnp.zeros((2, shift_ref.shape[1]), F32)], axis=0
+    )
+    plain_ref[...] = table
+    for k, part in enumerate(split3(table)):
+        table_ref[k * 32 : (k + 1) * 32, :] = part
     for k, part in enumerate(split3(minv_ref[...])):
         m3_ref[k * 32 : (k + 1) * 32, :] = part
     node_parts = split3(nodes_ref[...] * CROSS)
@@ -358,7 +359,7 @@
             src_ref=g2_ref.at[rows],
             dst_ref=g2_ref.at[rows],
             send_sem=sems.at[5],
-            recv_sem=sems.at[6],
+            recv_sem=sems.at[6 if near[k] else 11],
             device_id=device,
             device_id_type=MESH,
         )
@@ -457,10 +458,16 @@
     copies5 = [fifth_copy(k, *d) for k, d in enumerate([(0, 0)] + plane)]
     copies5[0].start()
     every3.wait_send()
-    generate_range(3, 7)
-    every4.wait_recv()
-    for copy in copies5[1:]:
-        copy.start()
+    generate_range(3, 6)
+    all_rows(g2_ref, NZ * sum(near), 5, 6).wait_recv()
+    for copy, close in zip(copies5[1:], near):
+        if close:
+            copy.start()
+    generate_range(6, 7)
+    all_rows(g2_ref, NZ * (len(near) - sum(near)), 5, 11).wait_recv()
+    for copy, close in zip(copies5[1:], near):
+        if not close:
+            copy.start()
     every4.wait_send()
     generate_range(7, 8)
     turned = gp_ref[...].T
@@ -571,7 +578,7 @@
 
         pl.run_scoped(scoped, *[pltpu.ACC(u % 2)((96, 256), F32) for u in range(count)])
 
-    gather_stage(chord_points, 10)
+    gather_stage(chord_points, 8)
 
     derivative = lobatto_derivative()
 
@@ -732,15 +739,15 @@
     stores = [pltpu.make_async_copy(b, c, sem.at[k + 2]) for k, (_, b, c) in enumerate(pairs)]
     for copy in loads:
         copy.start()
+    for k in range(2):
+        loads[k].wait()
+        stores[k].start()
     packed.wait()
     for t in range(4):
         for a in range(4):
             value = packed_ref[t, a]
             for q in range(4):
                 face_ref[t, :, a * 4 + q, :] = value[0:5, q * 32 : (q + 1) * 32]
-    for k in range(2):
-        loads[k].wait()
-        stores[k].start()
     stores.append(pltpu.make_async_copy(face_ref, face_out, sem.at[4]))
     stores[2].start()
     for copy in stores:
@@ -799,7 +806,7 @@
             pltpu.VMEM((2, 64, 8, 128), F32),
             pltpu.VMEM((4, 4, 8, 128), F32),
             pltpu.VMEM((4, 4, 8, 128), F32),
-            dma((11,)),
+            dma((12,)),
             dma((7,)),
             dma((10,)),
             dma((2,)),

time: 60.2 us -> 60.3 us (level)
  no operation moved by 1% of the time
where the time goes in v5:
time: 60.3 us; the launch traced here: 60.2 us
  Pallas kernels  59.3 us (98%)
  between operations  0.82 us (1%)
    pallas_call x1, Pallas kernels, on_device(): pl.pallas_call(kernel, out_shape=(jax.ShapeDtypeStruct((5, 64, 128), F32)...  57.1 us
    pallas_call x1, Pallas kernels, on_device(): pl.pallas_call(finish, out_shape=(jax.ShapeDtypeStruct((5, 64, 128), F32)...  2.19 us

profile of v5, /device:TPU:1, one launch (start us, length us, event | category | flops | bytes accessed | tf_op | source)
XLA Modules:
  0.0 60.2 jit_solution(16803093060062662301)
XLA Ops:
  0.6 57.1 %wing.1 = (f32[5,64,128]{2,1,0:T(8,128)}, f32[5,3,64,128]{3,2,1,0:T(8,128)}, f32[4,4,8,128]{3,2,1,0:T(8,128)}) custom-call(s32[1,32]{1,0:T(1,128)} %bitcast.6, f32[3,32]{1,0:T(4,128)} %ctrl_in.1, f32[3,2048]{1,0:T(4,128)} %nodes_in.1, f32[15,1024]{1,0:T(8,128)} %shift_in.1, f32[15,1024]{1,0:T(8,128)} %speed_in.1, f32[32,8192]{1,0:T(8,128)} %minv_in.1, ...), custom_call_target="tpu_custom_call" | custom-call | tf_op jit(solution)/shard_map/wing/pallas_call | solution.py:763
  57.8 2.2 %wing_end.1 = (f32[5,64,128]{2,1,0:T(8,128)}, f32[5,3,64,128]{3,2,1,0:T(8,128)}, f32[4,5,16,32]{3,2,1,0:T(8,128)}) custom-call(f32[5,64,128]{2,1,0:T(8,128)} %get-tuple-element.9.det_in, f32[5,3,64,128]{3,2,1,0:T(8,128)} %get-tuple-element.10.flux_in, f32[4,4,8,128]{3,2,1,0:T(8,128)} %get-tuple-element.11.packed_in), custom_call_target="tpu_custom_call" | custom-call | tf_op jit(solution)/shard_map/wing_end/pallas_call | solution.py:830

commit v6 on v5

--- a/solution.py
+++ b/solution.py
@@ -210,6 +210,34 @@
     copies1 = [first_copy(k, line_device(*d)) for k, d in enumerate(line)]
     for copy in copies1:
         copy.start()
+    def all_rows(ref, count, sent, received):
+        return pltpu.make_async_remote_copy(
+            src_ref=ref.at[pl.ds(0, count)],
+            dst_ref=ref.at[pl.ds(0, count)],
+            send_sem=sems.at[sent],
+            recv_sem=sems.at[received],
+            device_id=partner,
+            device_id_type=MESH,
+        )
+
+    every1 = all_rows(g1_ref, len(line), 0, 1)
+    every2 = all_rows(g1_ref, len(plane) * GROUP, 2, 3)
+    every1.wait_recv()
+
+    def second_copy(k, device):
+        rows = pl.ds(group * GROUP, GROUP)
+        return pltpu.make_async_remote_copy(
+            src_ref=g1_ref.at[rows],
+            dst_ref=g1_ref.at[rows],
+            send_sem=sems.at[2],
+            recv_sem=sems.at[3],
+            device_id=device,
+            device_id_type=MESH,
+        )
+
+    copies2 = [second_copy(k, plane_device(*d)) for k, d in enumerate(plane)]
+    for copy in copies2:
+        copy.start()
     for copy in loads[2:]:
         copy.wait()
     table = jnp.concatenate(
@@ -224,34 +252,6 @@
     nb_ref[...] = jnp.concatenate(
         [node_parts[part].astype(F32) for _, part in PAIRS] + [jnp.zeros((14, 2048), F32)], axis=0
     ).astype(BF16)
-    def all_rows(ref, count, sent, received):
-        return pltpu.make_async_remote_copy(
-            src_ref=ref.at[pl.ds(0, count)],
-            dst_ref=ref.at[pl.ds(0, count)],
-            send_sem=sems.at[sent],
-            recv_sem=sems.at[received],
-            device_id=partner,
-            device_id_type=MESH,
-        )
-
-    every1 = all_rows(g1_ref, len(line), 0, 1)
-    every2 = all_rows(g1_ref, len(plane) * GROUP, 2, 3)
-    every1.wait_recv()
-
-    def second_copy(k, device):
-        rows = pl.ds(group * GROUP, GROUP)
-        return pltpu.make_async_remote_copy(
-            src_ref=g1_ref.at[rows],
-            dst_ref=g1_ref.at[rows],
-            send_sem=sems.at[2],
-            recv_sem=sems.at[3],
-            device_id=device,
-            device_id_type=MESH,
-        )
-
-    copies2 = [second_copy(k, plane_device(*d)) for k, d in enumerate(plane)]
-    for copy in copies2:
-        copy.start()
     every1.wait_send()
     every2.wait_recv()
     every2.wait_send()

time: 60.3 us -> 60.3 us (level)
  no operation moved by 1% of the time
where the time goes in v6:
time: 60.3 us; the launch traced here: 60.2 us
  Pallas kernels  59.3 us (98%)
  between operations  0.82 us (1%)
    pallas_call x1, Pallas kernels, on_device(): pl.pallas_call(kernel, out_shape=(jax.ShapeDtypeStruct((5, 64, 128), F32)...  57.1 us
    pallas_call x1, Pallas kernels, on_device(): pl.pallas_call(finish, out_shape=(jax.ShapeDtypeStruct((5, 64, 128), F32)...  2.19 us

profile of v6, /device:TPU:1, one launch (start us, length us, event | category | flops | bytes accessed | tf_op | source)
XLA Modules:
  0.0 60.2 jit_solution(6021713985459393694)
XLA Ops:
  0.6 57.1 %wing.1 = (f32[5,64,128]{2,1,0:T(8,128)}, f32[5,3,64,128]{3,2,1,0:T(8,128)}, f32[4,4,8,128]{3,2,1,0:T(8,128)}) custom-call(s32[1,32]{1,0:T(1,128)} %bitcast.6, f32[3,32]{1,0:T(4,128)} %ctrl_in.1, f32[3,2048]{1,0:T(4,128)} %nodes_in.1, f32[15,1024]{1,0:T(8,128)} %shift_in.1, f32[15,1024]{1,0:T(8,128)} %speed_in.1, f32[32,8192]{1,0:T(8,128)} %minv_in.1, ...), custom_call_target="tpu_custom_call" | custom-call | tf_op jit(solution)/shard_map/wing/pallas_call | solution.py:763
  57.8 2.2 %wing_end.1 = (f32[5,64,128]{2,1,0:T(8,128)}, f32[5,3,64,128]{3,2,1,0:T(8,128)}, f32[4,5,16,32]{3,2,1,0:T(8,128)}) custom-call(f32[5,64,128]{2,1,0:T(8,128)} %get-tuple-element.9.det_in, f32[5,3,64,128]{3,2,1,0:T(8,128)} %get-tuple-element.10.flux_in, f32[4,4,8,128]{3,2,1,0:T(8,128)} %get-tuple-element.11.packed_in), custom_call_target="tpu_custom_call" | custom-call | tf_op jit(solution)/shard_map/wing_end/pallas_call | solution.py:830
